TPU v7x, 128 devices: a whole 4x4x4 slice. The times are simulated.
128 devices in a mesh: ay: 8 (over x, core), ax: 16 (over y, z).
Axes of the slice: x: 4, y: 4, z: 4, core: 2. Of those that a mesh axis runs over, the one named last changes fastest.
Arguments:
- gaseous_model: float32 [4, 4096, 4096], P(None, 'ay', 'ax'), may hold values from -6 to 6
- forcing_boundary: float32 [4, 4096, 4096], P(None, 'ay', 'ax'), may hold values from -16 to 16, as said below
- relaxation_strength_profile: float32 [4], replicated, may hold values from 0.2 to 1
- bottom_exchange_aloft: bfloat16 [8, 4096, 4096], P(None, 'ay', 'ax'), may hold values from -6 to 6
- exchange_bottom_sensitivity: float32 [8], replicated, may hold values from -1 to 1
- terrain_skin_warmth: bfloat16 [4096, 4096], P('ay', 'ax'), may hold values from -6 to 6
- tile_processor_home: int32 [16384], replicated, may hold values from 0 to 128, as said below
- marine_place_warmth: float32 [16384, 2304], P(('ay', 'ax')), may hold values from -6 to 6
- warming_coefficient: float32 [8], replicated, may hold values from -0.5 to 0.5
Outputs:
- atmosphere_out: float32 [4, 4096, 4096], P(None, 'ay', 'ax')
- ocean_flux: bfloat16 [16384, 8, 2304], P(('ay', 'ax'))
- ocean_sst_out: float32 [16384, 2304], P(('ay', 'ax'))
- surface_temp: float32 [4096, 4096], P('ay', 'ax')
Inputs may be any that keep to these rules, and one draw needn't show every extreme that they name: `forcing_boundary`: smooth large-scale patterns with cell-to-cell noise. `tile_processor_home`: 128 marks an all-land block that no ocean device holds. Among the 128 blocks of one tile at most 2 have the same owner, and some tile has exactly 2 with one owner. An ocean device holds at most 128 blocks, and some device holds exactly 128.
All inputs are finite; a program needn't handle non-finite values.
Results may differ from a plain program's by a relative error of at most 0.0037.
Values may be sent and summed in bfloat16 or wider, within the bound.
No kernel may reach another device: no remote copies, remote signals or barrier semaphores. Data moves between devices by JAX's collectives and lax.ppermute only.
A program may use at most 192 MiB of HBM per device.

v0:
```python
import math

import jax
import jax.numpy as jnp
from jax import lax
from jax.sharding import PartitionSpec as P

GRID = 4096
KMAX = 32
EXCHANGE_KINDS = 8
ABLOCK = 32
MARINE_TILE_EDGE = 48
GAS_PATCH_TOTAL = 1024
MARINE_PATCHES = 2304


highest_accuracy = lax.Precision.HIGHEST


def over_pieces(value, axis):
    return lax.all_gather(value, axis).sum(0)


def spectral_basis(length, offset, number, waves_top):
    points = offset + jnp.arange(number, dtype=jnp.int32)
    wavenumbers = jnp.arange(1, waves_top + 1, dtype=jnp.int32)
    phases = points[:, None] * wavenumbers[None, :] % length
    angles = phases.astype(jnp.float32) * (2.0 * math.pi / length)
    constant = jnp.full((number, 1), math.sqrt(1.0 / length), jnp.float32)
    factor = math.sqrt(2.0 / length)
    return jnp.concatenate([constant, factor * jnp.cos(angles), factor * jnp.sin(angles)], axis=1)


def intersection_table():
    ocean_index = jnp.arange(MARINE_TILE_EDGE, dtype=jnp.int32)[:, None]
    air_index = jnp.arange(ABLOCK, dtype=jnp.int32)[None, :]
    upper_edge = jnp.minimum(2 * ocean_index + 2, 3 * air_index + 3)
    lower_edge = jnp.maximum(2 * ocean_index, 3 * air_index)
    return jnp.maximum(upper_edge - lower_edge, 0).astype(jnp.float32)


def kron_table(weights):
    ocean_side, air_side = weights.shape
    paired = weights[:, None, :, None] * weights[None, :, None, :]
    return paired.reshape(ocean_side * ocean_side, air_side * air_side)


def body(
    gaseous_model,
    forcing_boundary,
    relaxation_strength_profile,
    bottom_exchange_aloft,
    exchange_bottom_sensitivity,
    terrain_skin_warmth,
    tile_processor_home,
    marine_place_warmth,
    warming_coefficient,
):
    rows_ay = lax.axis_size("ay")
    cols_ax = lax.axis_size("ax")
    processor_roster = rows_ay * cols_ax
    device_id = lax.axis_index("ay") * cols_ax + lax.axis_index("ax")
    level_count, tile_rows, tile_cols = gaseous_model.shape
    block_rows = tile_rows // ABLOCK
    block_cols = tile_cols // ABLOCK
    processor_portion = block_rows * block_cols
    capacity = 2 * processor_portion // processor_roster
    block_total = processor_roster * processor_portion
    basis_rows = spectral_basis(GRID, lax.axis_index("ay") * tile_rows, tile_rows, KMAX)
    basis_cols = spectral_basis(GRID, lax.axis_index("ax") * tile_cols, tile_cols, KMAX)
    departure = forcing_boundary - gaseous_model
    along_cols = jnp.einsum("lyx,xn->lyn", departure, basis_cols, precision=highest_accuracy)
    partial_sum = jnp.einsum("ym,lyn->lmn", basis_rows, along_cols, precision=highest_accuracy)
    coefficients = over_pieces(partial_sum, ("ay", "ax"))
    rows_back = jnp.einsum("ym,lmn->lyn", basis_rows, coefficients, precision=highest_accuracy)
    filtered = jnp.einsum("lyn,xn->lyx", rows_back, basis_cols, precision=highest_accuracy)
    advanced_condition = gaseous_model + relaxation_strength_profile[:, None, None] * filtered
    flux_air = (
        bottom_exchange_aloft.astype(jnp.float32)
        + exchange_bottom_sensitivity[:, None, None] * advanced_condition[level_count - 1]
    ).astype(jnp.bfloat16)
    air_blocks = flux_air.reshape(EXCHANGE_KINDS, block_rows, ABLOCK, block_cols, ABLOCK)
    air_blocks = air_blocks.transpose(1, 3, 0, 2, 4).reshape(
        processor_portion, EXCHANGE_KINDS, GAS_PATCH_TOTAL
    )
    owners = tile_processor_home.reshape(processor_roster, processor_portion)
    earlier = jnp.arange(processor_portion)[:, None] > jnp.arange(processor_portion)[None, :]
    matching = owners[:, :, None] == owners[:, None, :]
    within = jnp.sum(matching & earlier[None], axis=2)
    own_owner = lax.dynamic_index_in_dim(owners, device_id, 0, keepdims=False)
    own_within = lax.dynamic_index_in_dim(within, device_id, 0, keepdims=False)
    is_wet = own_owner < processor_roster
    target = jnp.where(is_wet, own_owner * capacity + own_within, processor_roster * capacity)
    source_row = (
        jnp.full((processor_roster * capacity,), -1, jnp.int32)
        .at[target]
        .set(jnp.arange(processor_portion, dtype=jnp.int32), mode="drop")
    )
    filled = source_row >= 0
    pick_rows = jnp.maximum(source_row, 0)
    is_mine = tile_processor_home == device_id
    my_blocks = jnp.nonzero(is_mine, size=processor_portion, fill_value=block_total)[0].astype(
        jnp.int32
    )
    possessed_indicator = my_blocks < block_total
    clipped = jnp.minimum(my_blocks, block_total - 1)
    arrival = (clipped // processor_portion * capacity + within.reshape(-1)[clipped]).astype(
        jnp.int32
    )
    forward_matrix = kron_table(intersection_table() / 2.0).T.astype(jnp.bfloat16)
    return_matrix = kron_table(intersection_table() / 3.0)
    regridded = jnp.dot(
        air_blocks.reshape(processor_portion * EXCHANGE_KINDS, GAS_PATCH_TOTAL),
        forward_matrix,
        preferred_element_type=jnp.float32,
    )
    regridded = regridded.astype(jnp.bfloat16).reshape(
        processor_portion, EXCHANGE_KINDS, MARINE_PATCHES
    )
    outgoing = jnp.where(filled[:, None, None], regridded[pick_rows], jnp.zeros((), jnp.bfloat16))
    incoming = lax.all_to_all(outgoing, ("ay", "ax"), split_axis=0, concat_axis=0, tiled=True)
    arrived = incoming[arrival]
    marine_exchange_mesh = jnp.where(
        possessed_indicator[:, None, None], arrived, jnp.zeros((), jnp.bfloat16)
    )
    marine_warming = jnp.zeros((processor_portion, MARINE_PATCHES), jnp.float32)
    for field_index in range(EXCHANGE_KINDS):
        marine_warming = marine_warming + warming_coefficient[field_index] * marine_exchange_mesh[
            :, field_index
        ].astype(jnp.float32)
    renewed_marine_warmth = jnp.where(
        possessed_indicator[:, None], marine_place_warmth + marine_warming, 0.0
    )
    sent_back_entries = jnp.dot(
        renewed_marine_warmth,
        return_matrix,
        precision=highest_accuracy,
        preferred_element_type=jnp.float32,
    )
    back_target = jnp.where(possessed_indicator, arrival, processor_roster * capacity)
    back_slot = (
        jnp.full((processor_roster * capacity,), -1, jnp.int32)
        .at[back_target]
        .set(jnp.arange(processor_portion, dtype=jnp.int32), mode="drop")
    )
    present = back_slot >= 0
    outgoing_back = jnp.where(present[:, None], sent_back_entries[jnp.maximum(back_slot, 0)], 0.0)
    home_rows = lax.all_to_all(outgoing_back, ("ay", "ax"), split_axis=0, concat_axis=0, tiled=True)
    land_blocks = terrain_skin_warmth.reshape(block_rows, ABLOCK, block_cols, ABLOCK).transpose(
        0, 2, 1, 3
    )
    land_blocks = land_blocks.reshape(processor_portion, GAS_PATCH_TOTAL).astype(jnp.float32)
    ocean_blocks = home_rows[jnp.minimum(target, processor_roster * capacity - 1)]
    surface_blocks = jnp.where(is_wet[:, None], ocean_blocks, land_blocks)
    bottom_quantity = (
        surface_blocks.reshape(block_rows, block_cols, ABLOCK, ABLOCK)
        .transpose(0, 2, 1, 3)
        .reshape(tile_rows, tile_cols)
    )
    return (advanced_condition, marine_exchange_mesh, renewed_marine_warmth, bottom_quantity)


def solution(mesh):
    return jax.shard_map(
        body,
        mesh=mesh,
        in_specs=(
            P(None, "ay", "ax"),
            P(None, "ay", "ax"),
            P(),
            P(None, "ay", "ax"),
            P(),
            P("ay", "ax"),
            P(),
            P(("ay", "ax"), None),
            P(),
        ),
        out_specs=(
            P(None, "ay", "ax"),
            P(("ay", "ax"), None, None),
            P(("ay", "ax"), None),
            P("ay", "ax"),
        ),
        check_vma=False,
    )
```

profile of v0, /device:TPU:1, one launch (start us, length us, event | category | flops | bytes accessed | tf_op | source)
XLA Modules:
  0.0 403.0 jit_solution(5744967799711025038)
XLA Ops:
  7.3 0.2 cosine_multiply_fusion.1
  7.5 0.3 cosine_multiply_fusion
  7.8 4.4 %fusion.2 = f32[4,512,65]{1,2,0:T(8,128)S(1)} fusion(f32[4,512,256]{2,1,0:T(8,128)} %param.10, f32[4,512,256]{2,1,0:T(8,128)} %param.9, f32[256,32]{0,1:T(8,128)S(1)} %get-tuple-element.20, f32[256,32]{0,1:T(8,128)S(1)} %get-tuple-element.19, f32[65]{0:T(128)S(1)} %pad.3.clone), kind=kOutput, calls=%fused_computation.20 | convolution fusion | flops 409502208 | bytes 4792580 | tf_op jit(solution)/shard_map/lyx,xn->lyn/dot_general | solution.py:72
  12.3 0.7 convolution_bitcast_fusion.1
  13.0 0.8 copy.70
  13.8 0.1 convert_multiply_fusion
  13.9 7.6 %multiply_convert_fusion = bf16[48,48,32,32]{1,0,3,2:T(8,128)(2,1)} fusion(f32[48,32]{0,1:T(8,128)S(1)} %get-tuple-element.18), kind=kLoop, calls=%fused_computation.8 | loop fusion | flops 4718592 | bytes 4724736 | tf_op jit(solution)/shard_map/convert_element_type | solution.py:110
  21.5 18.0 %convert_element_type.100 = bf16[2304,1024]{0,1:T(8,128)(2,1)} reshape(bf16[48,48,32,32]{1,0,3,2:T(8,128)(2,1)} %multiply_convert_fusion) | data formatting | bytes 9437184 | tf_op jit(solution)/shard_map/convert_element_type | solution.py:110
  39.6 5.1 %convert_reduce_fusion = s32[128,128]{1,0:T(8,128)S(1)} fusion(s32[128,128]{1,0:T(8,128)S(1)} %bitcast.72, pred[128,128]{1,0:T(8,128)(4,1)S(1)} %iota_compare_fusion.1), kind=kLoop, calls=%fused_computation.12 | loop fusion | flops 8372224 | bytes 147456 | tf_op jit(solution)/shard_map/reduce_sum | solution.py:89
  44.7 0.1 copy.76
  44.8 0.1 fusion.19
  45.0 14.7 %scatter_custom_fusion.1 = s32[256]{0:T(256)S(1)} fusion(s32[128]{0:T(128)S(1)} %get-tuple-element.11, s32[128]{0:T(128)S(1)} %iota.73, s32[]{:T(128)} %constant.131.clone.1), kind=kCustom, calls=%fused_computation.112 | custom fusion | bytes 1028 | tf_op jit(solution)/shard_map/scatter | solution.py:97
  59.7 40.9 %all-gather.3.cloned.1.call-done = f32[512,65,65]{2,1,0:T(8,128)} async-done(((f32[4,65,65]{2,1,0:T(8,128)}), f32[512,65,65]{2,1,0:T(8,128)}) %all-gather.3.cloned.1.call-update) | async-done | bytes 8652816 | tf_op jit(solution)/shard_map/all_gather | solution.py:21
  100.6 7.9 %reduce_sum.27 = f32[4,65,65]{2,1,0:T(8,128)S(1)} reduce(f32[128,4,65,65]{3,2,1,0:T(8,128)} %bitcast.70, f32[]{:T(128)} %constant.126.clone.1), dimensions={0}, to_apply=%region_0.1 | reduce | flops 2146300 | bytes 8720404
  108.4 0.7 convolution_bitcast_fusion
  109.2 2.0 multiply_add_fusion
  111.2 1.3 copy-done.4
  112.6 0.8 add_convert_fusion
  113.4 6.2 %reshape.638 = bf16[8,16,32,8,32]{4,3,2,1,0:T(8,128)(2,1)} reshape(bf16[8,512,256]{2,1,0:T(8,128)(2,1)S(1)} %add_convert_fusion) | data formatting | bytes 4194304 | tf_op jit(solution)/shard_map/reshape | solution.py:82
  119.6 9.1 %copy.90 = bf16[8,16,32,8,32]{4,2,0,3,1:T(8,128)(2,1)} copy(bf16[8,16,32,8,32]{4,3,2,1,0:T(8,128)(2,1)} %reshape.638) | data formatting | bytes 4194304 | tf_op jit(solution)/shard_map/reshape | solution.py:82
  128.7 11.3 %reshape_reshape.3 = bf16[1024,1024]{1,0:T(8,128)(2,1)S(1)} reshape(bf16[16,8,8,32,32]{4,3,2,1,0:T(8,128)(2,1)} %bitcast.69) | data formatting | bytes 4194304 | tf_op jit(solution)/shard_map/reshape;reshape | solution.py:113
  140.0 9.0 %fusion = bf16[128,8,2304]{2,1,0:T(8,128)(2,1)} fusion(bf16[1024,1024]{1,0:T(8,128)(2,1)S(1)} %reshape_reshape.3, bf16[2304,1024]{0,1:T(8,128)(2,1)} %convert_element_type.100), kind=kOutput, calls=%fused_computation.14 | convolution fusion | flops 4834197504 | bytes 11534336 | tf_op jit(solution)/shard_map/dot_general | solution.py:112
  149.0 11.6 %gather_fusion = bf16[256,8,2304]{2,1,0:T(8,128)(2,1)} fusion(bf16[128,8,2304]{2,1,0:T(8,128)(2,1)} %fusion, s32[1024]{0:T(1024)S(1)} %pad_clamp_fusion.4), kind=kCustom, calls=%fused_computation | custom fusion | bytes 18875392 | tf_op jit(solution)/shard_map/gather | solution.py:120
  160.5 8.1 %broadcast_select_fusion = bf16[256,8,2304]{2,1,0:T(8,128)(2,1)} fusion(bf16[256,8,2304]{2,1,0:T(8,128)(2,1)} %gather_fusion, pred[256]{0:T(512)(128)(4,1)S(1)} %broadcast_compare_fusion.2), kind=kLoop, calls=%fused_computation.10 | loop fusion | flops 4718592 | bytes 18874624 | tf_op jit(solution)/shard_map/jit(_where)/select_n | solution.py:120
  168.6 7.8 %all-to-all-start = ((bf16[256,8,2304]{2,1,0:T(8,128)(2,1)}), bf16[256,8,2304]{2,1,0:T(8,128)(2,1)}, u32[]{:S(2)}, u32[]{:S(2)}) async-start(bf16[256,8,2304]{2,1,0:T(8,128)(2,1)} %broadcast_select_fusion), calls=%async_computation | async-start | bytes 18874368 | tf_op jit(solution)/shard_map/all_to_all | solution.py:121
  176.4 0.6 convert_reduce_fusion.1
  177.0 0.1 copy.72
  177.1 0.2 reduce-window.12
  177.3 0.1 copy.73
  177.4 0.2 reduce-window.13
  177.6 0.1 slice_reduce_fusion
  177.7 0.1 copy.74
  177.8 0.1 compare_select_fusion
  177.9 113.4 %scatter_custom_fusion = s32[128]{0:T(128)S(1)} fusion(s32[16384]{0:T(1024)S(1)} %bitcast.76, s32[16384]{0:T(1024)S(1)} %broadcast.775, s32[]{:T(128)} %constant.118.clone.1), kind=kCustom, calls=%fused_computation.119 | custom fusion | flops 16384 | bytes 516 | tf_op jit(solution)/shard_map/scatter-add | solution.py:102
  291.3 0.1 copy.75
  291.5 0.2 select_n.217
  291.6 0.8 fusion.14
  292.4 1.1 gather_fusion.1
  293.6 0.1 copy.80
  293.7 11.2 %broadcast_multiply_fusion = f32[48,48,32,32]{1,0,3,2:T(8,128)} fusion(f32[48,32]{0,1:T(8,128)S(1)} %get-tuple-element.17), kind=kLoop, calls=%fused_computation.9 | loop fusion | flops 2359296 | bytes 9443328 | tf_op jit(solution)/shard_map/mul | solution.py:44
  304.9 20.6 %mul.295 = f32[2304,1024]{0,1:T(8,128)} reshape(f32[48,48,32,32]{1,0,3,2:T(8,128)} %broadcast_multiply_fusion) | data formatting | bytes 18874368 | tf_op jit(solution)/shard_map/mul | solution.py:44
  325.5 0.9 fusion.18
  326.3 1.4 scatter_custom_fusion.2
  327.7 0.2 broadcast_in_dim.134
  328.0 0.7 fusion.39
  328.6 0.7 fusion.32
  329.3 6.8 %gather_fusion.2 = bf16[128,8,2304]{2,1,0:T(8,128)(2,1)} fusion(bf16[256,8,2304]{2,1,0:T(8,128)(2,1)} %all-to-all-done, s32[1024]{0:T(1024)S(1)} %pad_clamp_fusion.2), kind=kCustom, calls=%fused_computation.2 | custom fusion | bytes 9437696 | tf_op jit(solution)/shard_map/gather | solution.py:122
  336.1 4.3 %copy_select_fusion = bf16[128,8,2304]{2,0,1:T(8,128)(2,1)S(1)} fusion(bf16[128,8,2304]{2,1,0:T(8,128)(2,1)} %gather_fusion.2, pred[128]{0:T(512)(128)(4,1)S(1)} %fusion.32), kind=kLoop, calls=%fused_computation.15 | loop fusion | flops 2359296 | bytes 9437312 | tf_op jit(solution)/shard_map/jit(_where)/select_n | solution.py:123
  340.5 6.0 %fusion.4 = f32[128,2304]{1,0:T(8,128)S(1)} fusion(f32[128,2304]{1,0:T(8,128)S(1)} %copy-done.6, bf16[128,8,2304]{2,0,1:T(8,128)(2,1)S(1)} %copy_select_fusion, f32[]{:T(128)} %bitcast.23, f32[]{:T(128)} %bitcast.22, f32[]{:T(128)} %bitcast.21, f32[]{:T(128)} %bitcast.20, f32[]{:T(128)} %bitcast.19, f32[]{:T(128)} %bitcast.18, f32[]{:T(128)} %bitcast.17, ...), kind=kLoop, calls=%fused_computation.24 | loop fusion | flops 7372800 | bytes 7078048 | tf_op jit(solution)/shard_map/jit(_where)/select_n | solution.py:131
  346.5 9.9 %fusion.40 = f32[128,1024]{1,0:T(8,128)S(1)} fusion(f32[128,2304]{1,0:T(8,128)S(1)} %fusion.4, f32[2304,1024]{0,1:T(8,128)S(1)} %copy-done.1), kind=kOutput, calls=%fused_computation.126 | convolution fusion | flops 3623878656 | bytes 11141120 | tf_op jit(solution)/shard_map/dot_general | solution.py:134
  356.4 1.1 gather_fusion.3
  357.4 0.8 gather.26
  358.2 1.5 broadcast_select_fusion.1
  359.7 9.8 %all-to-all-start.1 = ((f32[128,2,1024]{2,1,0:T(2,128)}), f32[128,2,1024]{2,1,0:T(2,128)S(1)}, u32[]{:S(2)}, u32[]{:S(2)}) async-start(f32[128,2,1024]{2,1,0:T(2,128)} %broadcast_select_fusion.1), calls=%async_computation.1 | async-start | bytes 2097152 | tf_op jit(solution)/shard_map/all_to_all | solution.py:148
  369.5 0.1 lt.137
  369.6 1.7 reshape.644
  371.4 7.1 %copy.85 = bf16[128,8,2304]{2,1,0:T(8,128)(2,1)} copy(bf16[128,8,2304]{2,0,1:T(8,128)(2,1)} %copy-done) | data formatting | bytes 9437184
  378.5 10.0 %all-to-all-done.1 = f32[128,2,1024]{2,1,0:T(2,128)S(1)} async-done(((f32[128,2,1024]{2,1,0:T(2,128)}), f32[128,2,1024]{2,1,0:T(2,128)S(1)}, u32[]{:S(2)}, u32[]{:S(2)}) %all-to-all-start.1) | async-done | bytes 1048608 | tf_op jit(solution)/shard_map/all_to_all | solution.py:148
  388.5 0.7 all_to_all.11
  389.2 0.8 gather_fusion.4
  390.0 0.7 gather.28
  390.7 2.2 fusion.1
  393.0 1.6 copy.84
  394.6 1.4 reshape.641
  (51 shorter events, 0.3 us)
Async XLA Ops:
  7.2 93.4 %all-gather.3.cloned.1.call-start = ((), (), s32[]{:S(2)}) async-start(), calls=%async_computation.2 | async-start | bytes 19021824 | tf_op jit(solution)/shard_map/all_gather | solution.py:21
  21.5 18.0 %copy-start.7 = (s32[16384]{0:T(1024)S(1)}, s32[16384]{0:T(1024)}, u32[]{:S(2)}) copy-start(s32[16384]{0:T(1024)} %param.15) | copy-start | bytes 196612
  100.6 8.6 %copy-start.2 = (f32[4,512,256]{2,1,0:T(8,128)S(1)}, f32[4,512,256]{2,1,0:T(8,128)}, u32[]{:S(2)}) copy-start(f32[4,512,256]{2,1,0:T(8,128)} %param.9) | copy-start | bytes 6291460
  100.6 8.6 %copy-start.11 = (f32[4]{0:T(128)S(1)}, f32[4]{0:T(128)}, u32[]{:S(2)}) copy-start(f32[4]{0:T(128)} %param.11) | copy-start | bytes 52
  109.2 3.4 copy-start.5
  109.2 3.4 copy-start.10
  111.2 1.3 copy-start.4
  168.6 160.7 %all-to-all-start = ((bf16[256,8,2304]{2,1,0:T(8,128)(2,1)}), bf16[256,8,2304]{2,1,0:T(8,128)(2,1)}, u32[]{:S(2)}, u32[]{:S(2)}) async-start(bf16[256,8,2304]{2,1,0:T(8,128)(2,1)} %broadcast_select_fusion), calls=%async_computation | async-start | bytes 18874368 | tf_op jit(solution)/shard_map/all_to_all | solution.py:121
  304.9 23.0 %copy-start.9 = (f32[8]{0:T(128)S(1)}, f32[8]{0:T(128)}, u32[]{:S(2)}) copy-start(f32[8]{0:T(128)} %param.17) | copy-start | bytes 100
  329.3 11.1 %copy-start.6 = (f32[128,2304]{1,0:T(8,128)S(1)}, f32[128,2304]{1,0:T(8,128)}, u32[]{:S(2)}) copy-start(f32[128,2304]{1,0:T(8,128)} %param.16) | copy-start | bytes 3538948
  336.1 10.3 %copy-start.1 = (f32[2304,1024]{0,1:T(8,128)S(1)}, f32[2304,1024]{0,1:T(8,128)}, u32[]{:S(2)}) copy-start(f32[2304,1024]{0,1:T(8,128)} %mul.295) | copy-start | bytes 28311556
  340.4 6.0 %copy-start = (bf16[128,8,2304]{2,0,1:T(8,128)(2,1)}, bf16[128,8,2304]{2,0,1:T(8,128)(2,1)S(1)}, u32[]{:S(2)}) copy-start(bf16[128,8,2304]{2,0,1:T(8,128)(2,1)S(1)} %copy_select_fusion) | copy-start | bytes 14155780
  346.4 9.9 %copy-start.3 = (f32[128,2304]{1,0:T(8,128)}, f32[128,2304]{1,0:T(8,128)S(1)}, u32[]{:S(2)}) copy-start(f32[128,2304]{1,0:T(8,128)S(1)} %fusion.4) | copy-start | bytes 3538948
  358.2 11.4 %copy-start.8 = (bf16[512,256]{1,0:T(8,128)(2,1)S(1)}, bf16[512,256]{1,0:T(8,128)(2,1)}, u32[]{:S(2)}) copy-start(bf16[512,256]{1,0:T(8,128)(2,1)} %param.14) | copy-start | bytes 786436
  359.7 28.8 %all-to-all-start.1 = ((f32[128,2,1024]{2,1,0:T(2,128)}), f32[128,2,1024]{2,1,0:T(2,128)S(1)}, u32[]{:S(2)}, u32[]{:S(2)}) async-start(f32[128,2,1024]{2,1,0:T(2,128)} %broadcast_select_fusion.1), calls=%async_computation.1 | async-start | bytes 2097152 | tf_op jit(solution)/shard_map/all_to_all | solution.py:148
Sparse Core Ops, SparseCore 0:
  13.9 86.5 all-gather.2
where the time goes:
time: 410 us; the launch traced here: 403 us
  other arithmetic  173 us (42%)
  local copies, waits for them, and re-layouts  121 us (30%)
  waiting for transfers between devices  50.9 us (12%)
  matrix products  26.7 us (7%)
  starting transfers between devices  17.6 us (4%)
  between operations  14.7 us (4%)
    scatter-add x1, other arithmetic, body(): jnp.nonzero(is_mine, size=processor_portion, fill_value=block_total)[0]  113 us
    all_gather x1, waiting for transfers between devices, over_pieces(): return lax.all_gather(value, axis).sum(0)  40.9 us
    mul x1, local copies, waits for them, and re-layouts, kron_table(): paired = weights[:, None, :, None] * weights[None, :, None, :]  20.6 us
    convert_element_type x1, local copies, waits for them, and re-layouts, body(): kron_table(intersection_table() / 2.0).T.astype(jnp.bfloat16)  18 us
    reshape x2, local copies, waits for them, and re-layouts, body(): flux_air.reshape(EXCHANGE_KINDS, block_rows, ABLOCK, block_cols, ABLOCK)  15.3 us
    scatter x1, local copies, waits for them, and re-layouts, body(): source_row = jnp.full((processor_roster * capacity,), -1, jnp.int32).at[t...  14.7 us
    gather x1, local copies, waits for them, and re-layouts, body(): regridded[pick_rows]  11.6 us
    another operation x1, local copies, waits for them, and re-layouts, body(): air_blocks.reshape(processor_portion * EXCHANGE_KINDS, GAS_PATCH_TOTAL)  11.3 us
  transfers between devices with their start and end apart: 3, of which 2 were waited for; matrix products, arithmetic and copies ran while one was open for 52% of the time, Pallas kernels for 0%

commit v1 on v0

v1 whole, which is shorter than its diff:
```python
import functools
import math

import jax
import jax.numpy as jnp
import numpy as np
from jax import lax
from jax.experimental import pallas as pl
from jax.experimental.pallas import tpu as pltpu
from jax.sharding import PartitionSpec as P

GRID = 4096
KMAX = 32
LEVELS = 4
FIELDS = 8
ABLOCK = 32
OBLOCK = 48
ACELLS = 1024
OCELLS = 2304
TILE_ROWS = 512
TILE_COLS = 256
BLOCK_ROWS = 16
BLOCK_COLS = 8
N_AX = 16
DEVICES = 128
SLOTS = 128
MODES = 64
CROWS = 72
MSG_ROWS = 72
F32 = jnp.float32
BF16 = jnp.bfloat16


def _split(x):
    hi = np.asarray(x, np.float32).astype(jnp.bfloat16)
    lo = (np.asarray(x, np.float64) - hi.astype(np.float64)).astype(jnp.bfloat16)
    return hi, lo


def _modes(points):
    k = np.arange(1, KMAX + 1)
    angle = (np.asarray(points)[:, None] * k[None, :] % GRID) * (2.0 * math.pi / GRID)
    factor = math.sqrt(2.0 / GRID)
    return np.concatenate([factor * np.cos(angle), factor * np.sin(angle)], axis=1)


def _intersection():
    o = np.arange(OBLOCK)[:, None]
    a = np.arange(ABLOCK)[None, :]
    return np.maximum(np.minimum(2 * o + 2, 3 * a + 3) - np.maximum(2 * o, 3 * a), 0).astype(np.float64)


@functools.cache
def _tables():
    hi, lo = _split(_modes(np.arange(GRID)))
    basis = np.concatenate([hi, lo], axis=1)
    inter = _intersection()
    kron = np.kron(inter, inter)
    forward = np.zeros((5, 256, 256), np.float32)
    for t, first in enumerate(FWD_FIRST):
        out = min(256, 1152 - 256 * t)
        forward[t, :, :out] = kron[256 * t : 256 * t + out, 128 * first : 128 * first + 256].T / 4.0
    back = np.zeros((4, 384, 128), np.float32)
    for j in range(4):
        back[j] = kron[256 * j : 256 * j + 384, 128 * j : 128 * j + 128]
    local = np.zeros((256, 128))
    for k in range(4):
        local[64 * k : 64 * k + 64, 32 * k : 32 * k + 32] = _modes(np.arange(ABLOCK)).T
    lhi, llo = _split(local)
    synth = np.concatenate([lhi, llo], axis=1)
    k = np.arange(1, KMAX + 1)
    alpha = (np.arange(128)[:, None] * ABLOCK * k[None, :] % GRID) * (2.0 * math.pi / GRID)
    c, s = np.cos(alpha), np.sin(alpha)
    turn = np.concatenate([c, c, c, c, s, -s, s, -s], axis=1).astype(np.float32)
    return basis, forward.astype(jnp.bfloat16), back.astype(jnp.bfloat16), synth, turn


FWD_FIRST = (0, 0, 1, 2, 2)


def _hilo(x):
    hi = x.astype(BF16)
    return hi, (x - hi.astype(F32)).astype(BF16)


def _mm(a, b):
    return jnp.dot(a, b, preferred_element_type=F32)


def _swap_groups(v, group):
    low2, even = group < 2, group % 2 == 0
    r = lambda x, n: pltpu.roll(x, n, 1)
    a0 = jnp.where(low2, v[0], r(v[2], 64))
    a2 = jnp.where(low2, r(v[0], 64), v[2])
    a1 = jnp.where(low2, v[1], r(v[3], 64))
    a3 = jnp.where(low2, r(v[1], 64), v[3])
    return (
        jnp.where(even, a0, r(a1, 32)),
        jnp.where(even, r(a0, 96), a1),
        jnp.where(even, a2, r(a3, 32)),
        jnp.where(even, r(a2, 96), a3),
    )


def _lane_group():
    return lax.broadcasted_iota(jnp.int32, (8, 128), 1) // 32


def _index_rows(owners, own, dev):
    lane = lax.broadcasted_iota(jnp.int32, (128, 128), 1)
    row = lax.broadcasted_iota(jnp.int32, (128, 128), 0)
    mine = owners == dev
    eq = mine.astype(F32)
    count = jnp.sum(eq, axis=1, keepdims=True)
    running = jnp.sum(_mm((row >= lane).astype(BF16), eq.astype(BF16)), axis=1, keepdims=True)
    before = (running <= lane.astype(F32)).astype(F32)
    tile = jnp.sum(before, axis=0, keepdims=True)
    base = jnp.sum(before * count, axis=0, keepdims=True)
    first = jnp.min(jnp.where(mine, lane, 127), axis=1, keepdims=True).astype(F32)
    last = jnp.max(jnp.where(mine, lane, 0), axis=1, keepdims=True).astype(F32)
    chosen = (row.astype(F32) == tile).astype(F32)
    first = jnp.sum(chosen * first, axis=0, keepdims=True)
    last = jnp.sum(chosen * last, axis=0, keepdims=True)
    tile_i = tile.astype(jnp.int32)
    nth = lane[:1] - base.astype(jnp.int32)
    held = tile_i < 128
    block = jnp.where(nth == 0, first, last).astype(jnp.int32)
    arrival = jnp.where(held, 2 * tile_i + nth, 0)
    block_row = jnp.where(held, (tile_i // N_AX) * BLOCK_ROWS + block // BLOCK_COLS, 0)
    block_col = jnp.where(held, (tile_i % N_AX) * BLOCK_COLS + block % BLOCK_COLS, 0)
    total = jnp.sum(held.astype(jnp.int32), axis=1, keepdims=True)
    own_b = jnp.broadcast_to(own, (128, 128))
    own_col = jnp.sum(jnp.where(row == lane, own_b, 0), axis=1, keepdims=True)
    earlier = jnp.where((own_col == own_b) & (row < lane), 1, 0)
    nth_own = jnp.sum(earlier, axis=0, keepdims=True)
    wet = own < DEVICES
    target = jnp.where(wet, 2 * own + nth_own, -1)
    total = jnp.broadcast_to(total, (1, 128))
    rows = jnp.concatenate([arrival, target, block_row, block_col, total, total, total, total], axis=0)
    pick = jnp.where((lane // 8 == row) & (jnp.broadcast_to(wet, (128, 128))), 1.0, 0.0)[:BLOCK_ROWS]
    lane2 = lax.broadcasted_iota(jnp.int32, (128, TILE_COLS), 1)
    row2 = lax.broadcasted_iota(jnp.int32, (128, TILE_COLS), 0)
    spread = (row2 % 8 == lane2 // ABLOCK).astype(BF16)
    return rows, _mm(pick.astype(BF16), spread)


def _pack_kernel(
    dev_s, sens_s, owners_r, own_r, air_r, low_r, marine_r, back_r, msg_r, idx_r, wet_r, field_s, home_s, idx_s, copy_sem
):
    b = pl.program_id(0)

    @pl.when(b == 0)
    def _():
        rows, wet = _index_rows(owners_r[...], own_r[...].reshape(1, 128), dev_s[0])
        idx_r[...] = rows
        wet_r[...] = wet
        copy = pltpu.make_async_copy(idx_r, idx_s, copy_sem)
        copy.start()
        for j in range(8):
            start = 1152 * (j // 4) + 256 * (j % 4)
            hi, lo = _hilo(marine_r[:, start : start + 384])
            part = (_mm(hi, back_r[j % 4]) + _mm(lo, back_r[j % 4])) * (1.0 / 9.0)
            home_s[pl.ds(j, SLOTS, stride=8), :] = part
        copy.wait()
        held = idx_s[4, 0]

        def put(s, carry):
            @pl.when(s < held)
            def _():
                at = pl.multiple_of(s * 8, 8)
                msg_r[idx_s[0, s], 64:72, :] = home_s[pl.ds(at, 8), :].astype(BF16)

            return carry

        lax.fori_loop(0, SLOTS, put, 0, unroll=8)

    group = _lane_group()
    low = low_r[0]
    for f in range(FIELDS):
        value = air_r[f].astype(F32) + sens_s[f] * low
        for h in range(2):
            field_s[h, 32 * f : 32 * f + 32, :] = value[:, 128 * h : 128 * h + 128]
    for h in range(2):
        out = [[] for _ in range(4)]
        for j in range(8):
            v = [field_s[h, pl.ds(4 * j + k, 8, stride=32), :] for k in range(4)]
            for c, w in enumerate(_swap_groups(v, group)):
                out[c].append(w)
        for c in range(4):
            target = idx_s[1, b * 8 + 4 * h + c]
            packed = jnp.concatenate(out[c], axis=0).astype(BF16)

            @pl.when(target >= 0)
            def _():
                msg_r[target, 0:64, :] = packed


def _pack(dev, sens, owners, own, air, model, marine, back):
    return pl.pallas_call(
        _pack_kernel,
        grid_spec=pltpu.PrefetchScalarGridSpec(
            num_scalar_prefetch=2,
            grid=(BLOCK_ROWS,),
            in_specs=[
                pl.BlockSpec((128, 128), lambda b, *_: (0, 0)),
                pl.BlockSpec((1, 1, 128), lambda b, d, s: (d[0], 0, 0)),
                pl.BlockSpec((FIELDS, ABLOCK, TILE_COLS), lambda b, *_: (0, b, 0)),
                pl.BlockSpec((1, ABLOCK, TILE_COLS), lambda b, *_: (LEVELS - 1, b, 0)),
                pl.BlockSpec((SLOTS, OCELLS), lambda b, *_: (0, 0)),
                pl.BlockSpec((4, 384, 128), lambda b, *_: (0, 0, 0)),
            ],
            out_specs=[
                pl.BlockSpec((2 * DEVICES, MSG_ROWS, 128), lambda b, *_: (0, 0, 0)),
                pl.BlockSpec((8, 128), lambda b, *_: (0, 0)),
                pl.BlockSpec((BLOCK_ROWS, TILE_COLS), lambda b, *_: (0, 0)),
            ],
            scratch_shapes=[
                pltpu.VMEM((2, FIELDS * ABLOCK, 128), F32),
                pltpu.VMEM((SLOTS * 8, 128), F32),
                pltpu.SMEM((8, 128), jnp.int32),
                pltpu.SemaphoreType.DMA(()),
            ],
        ),
        out_shape=[
            jax.ShapeDtypeStruct((2 * DEVICES, MSG_ROWS, 128), BF16),
            jax.ShapeDtypeStruct((8, 128), jnp.int32),
            jax.ShapeDtypeStruct((BLOCK_ROWS, TILE_COLS), F32),
        ],
        name="pack",
    )(dev, sens, owners, own, air, model, marine, back)


def _analyse_kernel(pos_s, model_r, forcing_r, rows_r, cols_r, out_r):
    d = forcing_r[0] - model_r[0]
    hi, lo = _hilo(d)
    along = _mm(hi, cols_r[...]) + _mm(lo, cols_r[...])
    along = along + pltpu.roll(along, 64, 1)
    mean = jnp.sum(d, axis=1, keepdims=True) * (1.0 / 64.0)
    lane = lax.broadcasted_iota(jnp.int32, (TILE_ROWS, 128), 1)
    along = jnp.where(lane < 64, along, jnp.where(lane == 64, mean, 0.0))
    hi, lo = _hilo(along)
    contract = (((0,), (0,)), ((), ()))
    both = lax.dot_general(rows_r[...], hi, contract, preferred_element_type=F32) + lax.dot_general(
        rows_r[...], lo, contract, preferred_element_type=F32
    )
    out_r[0:64, :] = both[0:64] + both[64:128]
    mean = jnp.sum(along, axis=0, keepdims=True) * (1.0 / 64.0)
    row = lax.broadcasted_iota(jnp.int32, (8, 128), 0)
    out_r[64:72, :] = jnp.where(row == 0, jnp.broadcast_to(mean, (8, 128)), 0.0)


def _analyse(pos, model, forcing, basis):
    return pl.pallas_call(
        _analyse_kernel,
        grid_spec=pltpu.PrefetchScalarGridSpec(
            num_scalar_prefetch=1,
            grid=(LEVELS,),
            in_specs=[
                pl.BlockSpec((1, TILE_ROWS, TILE_COLS), lambda l, p: (l, 0, 0)),
                pl.BlockSpec((1, TILE_ROWS, TILE_COLS), lambda l, p: (l, 0, 0)),
                pl.BlockSpec((TILE_ROWS, 128), lambda l, p: (p[0], 0)),
                pl.BlockSpec((TILE_COLS, 128), lambda l, p: (p[1], 0)),
            ],
            out_specs=pl.BlockSpec((CROWS, 128), lambda l, p: (l, 0)),
        ),
        out_shape=jax.ShapeDtypeStruct((LEVELS * CROWS, 128), F32),
        name="analyse",
    )(pos, model, forcing, basis, basis)


def _nudge_kernel(
    pos_s, strength_s, sens_s, warm_s, coef_r, rows_r, cols_r, model_r, air_r, land_r, wet_r, out_r, base_r, cols_s
):
    step = pl.program_id(0)
    lane = lax.broadcasted_iota(jnp.int32, (CROWS, 128), 1)

    @pl.when(step == 0)
    def _():
        contract = (((1,), (1,)), ((), ()))
        cols = cols_r[...]
        for l in range(LEVELS):
            coef = coef_r[CROWS * l : CROWS * l + CROWS, :]
            modes = jnp.where(lane < 64, coef, 0.0)
            hi, lo = _hilo(modes + pltpu.roll(modes, 64, 1))
            low, _ = _hilo(modes - jnp.where(lane < 64, hi.astype(F32), 0.0))
            t = lax.dot_general(hi, cols, contract, preferred_element_type=F32) + lax.dot_general(
                low, cols, contract, preferred_element_type=F32
            )
            mean = jnp.sum(jnp.where(lane == 64, coef, 0.0), axis=1, keepdims=True) * (1.0 / 64.0)
            t = (t + mean) * strength_s[l]
            hi, lo = _hilo(t[0:64])
            cols_s[l, 0:64, :] = hi
            cols_s[l, 64:128, :] = hi
            cols_s[l, 128:192, :] = lo
            cols_s[l, 192:256, :] = jnp.broadcast_to((t[64:72] * (1.0 / 64.0))[0:1], (64, TILE_COLS)).astype(BF16)
            c = t[64:65] * (1.0 / 64.0)
            chi, clo = _hilo(c)
            r = lax.broadcasted_iota(jnp.int32, (64, TILE_COLS), 0)
            full = jnp.where(r == 0, chi.astype(F32), jnp.where(r == 1, clo.astype(F32), 0.0))
            cols_s[l, 192:256, :] = full.astype(BF16)

    n = model_r.shape[1]
    rows = rows_r[...]
    lane_n = lax.broadcasted_iota(jnp.int32, (n, 128), 1)
    second = jnp.where(lane_n < 64, rows.astype(F32), jnp.where(lane_n < 66, 1.0, 0.0)).astype(BF16)
    left = jnp.concatenate([rows, second], axis=1)
    low = None
    for l in range(LEVELS):
        low = model_r[l] + _mm(left, cols_s[l])
        out_r[l] = low
    heat = None
    gain = 0.0
    for f in range(FIELDS):
        part = warm_s[f] * air_r[f].astype(F32)
        heat = part if heat is None else heat + part
        gain = gain + warm_s[f] * sens_s[f]
    heat = heat + gain * low
    row = lax.broadcasted_iota(jnp.int32, (n, TILE_COLS), 0)
    col = lax.broadcasted_iota(jnp.int32, (n, TILE_COLS), 1)
    partner = jnp.where(col % 2 == 0, pltpu.roll(heat, TILE_COLS - 1, 1), pltpu.roll(heat, 1, 1))
    heat = heat * (5.0 / 6.0) + partner * (1.0 / 6.0)
    partner = jnp.where(row % 2 == 0, pltpu.roll(heat, n - 1, 0), pltpu.roll(heat, 1, 0))
    heat = heat * (5.0 / 6.0) + partner * (1.0 / 6.0)
    for i in range(n // ABLOCK):
        at = slice(ABLOCK * i, ABLOCK * i + ABLOCK)
        wet = wet_r[pl.ds(step * (n // ABLOCK) + i, 1), :] > 0.5
        base_r[at, :] = jnp.where(wet, heat[at], land_r[at, :].astype(F32))


def _nudge(pos, strength, sens, warm, coef, basis, model, air, land, wet):
    n = 128
    per = TILE_ROWS // n
    return pl.pallas_call(
        _nudge_kernel,
        grid_spec=pltpu.PrefetchScalarGridSpec(
            num_scalar_prefetch=4,
            grid=(per,),
            in_specs=[
                pl.BlockSpec((LEVELS * CROWS, 128), lambda i, *_: (0, 0)),
                pl.BlockSpec((n, 128), lambda i, p, *_: (p[0] * per + i, 0)),
                pl.BlockSpec((TILE_COLS, 128), lambda i, p, *_: (p[1], 0)),
                pl.BlockSpec((LEVELS, n, TILE_COLS), lambda i, *_: (0, i, 0)),
                pl.BlockSpec((FIELDS, n, TILE_COLS), lambda i, *_: (0, i, 0)),
                pl.BlockSpec((n, TILE_COLS), lambda i, *_: (i, 0)),
                pl.BlockSpec((BLOCK_ROWS, TILE_COLS), lambda i, *_: (0, 0)),
            ],
            out_specs=[
                pl.BlockSpec((LEVELS, n, TILE_COLS), lambda i, *_: (0, i, 0)),
                pl.BlockSpec((n, TILE_COLS), lambda i, *_: (i, 0)),
            ],
            scratch_shapes=[pltpu.VMEM((LEVELS, 256, TILE_COLS), BF16)],
        ),
        out_shape=[
            jax.ShapeDtypeStruct((LEVELS, TILE_ROWS, TILE_COLS), F32),
            jax.ShapeDtypeStruct((TILE_ROWS, TILE_COLS), F32),
        ],
        name="nudge",
    )(pos, strength, sens, warm, coef, basis, basis, model, air, land, wet)


def _regrid_tiles(get):
    for half in range(2):
        for t, first in enumerate(FWD_FIRST):
            j = 4 * half + first
            yield 1152 * half + 256 * t, min(256, 1152 - 256 * t), t, j


def _held_kernel(idx_s, strength_s, coef_r, basis_r, synth_r, turn_r, fwd_r, out_r, plain_s, other_s, mean_s, left_s, cell_s):
    lane = lax.broadcasted_iota(jnp.int32, (CROWS, 128), 1)
    coef = coef_r[...] * strength_s[LEVELS - 1]
    modes = jnp.where(lane < 64, coef, 0.0)
    modes = modes + pltpu.roll(modes, 64, 1)
    swapped = jnp.where(lane % 64 < 32, pltpu.roll(modes, 96, 1), pltpu.roll(modes, 32, 1))
    mean = jnp.sum(jnp.where(lane == 64, coef, 0.0), axis=1, keepdims=True) * (1.0 / 64.0)
    mean = jnp.broadcast_to(mean, (CROWS, 128))
    right = jnp.concatenate([modes, swapped, mean], axis=1)
    hi, lo = _hilo(right[0:64])
    weights = jnp.concatenate([hi, hi, lo, jnp.zeros_like(lo)], axis=0)
    const = right[64:65] * (1.0 / 64.0)
    chunk = 512
    for i in range(GRID // chunk):
        rows = basis_r[chunk * i : chunk * i + chunk, :]
        left = jnp.concatenate([rows, rows], axis=1)
        table = _mm(left, weights) + const
        for n, ref in enumerate((plain_s, other_s, mean_s)):
            ref[chunk * i : chunk * i + chunk, :] = table[:, 128 * n : 128 * n + 128]
    lane = lax.broadcasted_iota(jnp.int32, (8, 128), 1)
    low = lane < 64
    group = lane // 32

    def slot(s, carry):
        start = idx_s[2, s] * ABLOCK
        turn = turn_r[pl.ds(idx_s[3, s], 1), :]
        plains, others, means = (
            [ref[pl.ds(start + k, 8, stride=4), :] for k in range(4)] for ref in (plain_s, other_s, mean_s)
        )
        at = pl.multiple_of(s * 8, 8)
        for p in range(2):
            plain = jnp.where(low, plains[2 * p], plains[2 * p + 1])
            other = jnp.where(low, others[2 * p], others[2 * p + 1])
            left_s[pl.ds(at, 8), 128 * p : 128 * p + 128] = plain * turn[:, 0:128] + other * turn[:, 128:256]
        m = jnp.where(group == 0, means[0], means[1])
        m = jnp.where(group < 2, m, jnp.where(group == 2, means[2], means[3]))
        cell_s[pl.ds(at, 8), :] = m
        return carry

    lax.fori_loop(0, SLOTS, slot, 0, unroll=4)
    hi, lo = _hilo(left_s[...])
    both = _mm(hi, synth_r[...])
    cell_s[...] = cell_s[...] + both[:, 0:128] + both[:, 128:256] + _mm(lo, synth_r[:, 0:128])
    tiles = [_hilo(cell_s[pl.ds(j, SLOTS, stride=8), :]) for j in range(8)]
    for at, width, t, j in _regrid_tiles(None):
        w = fwd_r[t][:, 0:width]
        hi = jnp.concatenate([tiles[j][0], tiles[j + 1][0]], axis=1)
        lo = jnp.concatenate([tiles[j][1], tiles[j + 1][1]], axis=1)
        out_r[:, at : at + width] = _mm(hi, w) + _mm(lo, w)


def _held(idx, strength, coef, basis, synth, turn, fwd):
    whole = lambda *shape: pl.BlockSpec(shape, lambda i, *_: (0,) * len(shape))
    return pl.pallas_call(
        _held_kernel,
        grid_spec=pltpu.PrefetchScalarGridSpec(
            num_scalar_prefetch=2,
            grid=(1,),
            in_specs=[
                pl.BlockSpec((CROWS, 128), lambda i, *_: (LEVELS - 1, 0)),
                whole(GRID, 128),
                whole(256, 256),
                whole(128, 256),
                whole(5, 256, 256),
            ],
            out_specs=whole(SLOTS, OCELLS),
            scratch_shapes=[
                pltpu.VMEM((GRID, 128), F32),
                pltpu.VMEM((GRID, 128), F32),
                pltpu.VMEM((GRID, 128), F32),
                pltpu.VMEM((SLOTS * 8, 256), F32),
                pltpu.VMEM((SLOTS * 8, 128), F32),
            ],
        ),
        out_shape=jax.ShapeDtypeStruct((SLOTS, OCELLS), F32),
        name="held",
    )(idx, strength, coef, basis, synth, turn, fwd)


OCEAN_STEP = 32


def _column(s_ref, n):
    row = lax.broadcasted_iota(jnp.int32, (8, 128), 0)
    v = jnp.zeros((8, 128), F32)
    for f in range(n):
        v = jnp.where(row == f, s_ref[f], v)
    return v


def _sum_rows(v, row):
    for shift, bit in ((4, 4), (2, 2), (1, 1)):
        keep = (row & bit) == 0
        half = len(v) // 2
        v = [
            jnp.where(keep, v[i], pltpu.roll(v[i + half], shift, 0))
            + jnp.where(keep, pltpu.roll(v[i], 8 - shift, 0), v[i + half])
            for i in range(half)
        ]
    return v[0]


def _ocean_kernel(idx_s, sens_s, warm_s, *refs):
    blocks = refs[:OCEAN_STEP]
    incr_r, marine_r, fwd_r, flux_r, sst_r = refs[OCEAN_STEP:]
    step = pl.program_id(0)
    held = idx_s[4, 0] - step * OCEAN_STEP
    sens = _column(sens_s, FIELDS)
    warm = _column(warm_s, FIELDS)
    tiles = [
        jnp.concatenate([blocks[q][0, 8 * j : 8 * j + 8, :] for q in range(OCEAN_STEP)], axis=0) for j in range(8)
    ]
    row = lax.broadcasted_iota(jnp.int32, (8, 128), 0)
    for at, width, t, j in _regrid_tiles(None):
        y = _mm(jnp.concatenate([tiles[j], tiles[j + 1]], axis=1), fwd_r[t][:, 0:width])
        for u in range(width // 128):
            cols = slice(at + 128 * u, at + 128 * u + 128)
            for g in range(OCEAN_STEP // 8):
                heats = []
                for q in range(8):
                    s = 8 * g + q
                    value = y[8 * s : 8 * s + 8, 128 * u : 128 * u + 128]
                    value = value + sens * jnp.broadcast_to(incr_r[s : s + 1, cols], (8, 128))
                    value = jnp.where(s < held, value, 0.0).astype(BF16)
                    flux_r[s, :, cols] = value
                    heats.append(value.astype(F32) * warm)
                heat = _sum_rows(heats, row)
                keep = row + 8 * g < held
                sst_r[8 * g : 8 * g + 8, cols] = jnp.where(keep, marine_r[8 * g : 8 * g + 8, cols] + heat, 0.0)


def _ocean(idx, sens, warm, incoming, incr, marine, fwd):
    def block(q):
        return pl.BlockSpec((1, 64, 128), lambda i, idx, *_: (idx[0, i * OCEAN_STEP + q], 0, 0))

    rows = lambda: pl.BlockSpec((OCEAN_STEP, OCELLS), lambda i, *_: (i, 0))
    return pl.pallas_call(
        _ocean_kernel,
        grid_spec=pltpu.PrefetchScalarGridSpec(
            num_scalar_prefetch=3,
            grid=(SLOTS // OCEAN_STEP,),
            in_specs=[block(q) for q in range(OCEAN_STEP)]
            + [rows(), rows(), pl.BlockSpec((5, 256, 256), lambda i, *_: (0, 0, 0))],
            out_specs=[pl.BlockSpec((OCEAN_STEP, FIELDS, OCELLS), lambda i, *_: (i, 0, 0)), rows()],
        ),
        out_shape=[
            jax.ShapeDtypeStruct((SLOTS, FIELDS, OCELLS), BF16),
            jax.ShapeDtypeStruct((SLOTS, OCELLS), F32),
        ],
        name="ocean",
    )(idx, sens, warm, *([incoming] * OCEAN_STEP), incr, marine, fwd)


def _surface_kernel(idx_s, back_r, base_r, wet_r, out_r, cell_s):
    group = _lane_group()

    def rows(b, carry):
        for h in range(2):
            v = [back_r[jnp.maximum(idx_s[1, b * 8 + 4 * h + c], 0)].astype(F32) for c in range(4)]
            for k, w in enumerate(_swap_groups(v, group)):
                cell_s[h, pl.ds(k, 8, stride=4), :] = w
        at = pl.multiple_of(b * ABLOCK, ABLOCK)
        wet = wet_r[pl.ds(b, 1), :] > 0.5
        cells = jnp.concatenate([cell_s[0], cell_s[1]], axis=1)
        out_r[pl.ds(at, ABLOCK), :] = base_r[pl.ds(at, ABLOCK), :] + jnp.where(wet, cells, 0.0)
        return carry

    lax.fori_loop(0, BLOCK_ROWS, rows, 0, unroll=2)


def _surface(idx, incoming, base, wet):
    whole = lambda *shape: pl.BlockSpec(shape, lambda i, *_: (0,) * len(shape))
    return pl.pallas_call(
        _surface_kernel,
        grid_spec=pltpu.PrefetchScalarGridSpec(
            num_scalar_prefetch=1,
            grid=(1,),
            in_specs=[
                pl.BlockSpec((2 * DEVICES, 8, 128), lambda i, *_: (0, 8, 0)),
                whole(TILE_ROWS, TILE_COLS),
                whole(BLOCK_ROWS, TILE_COLS),
            ],
            out_specs=whole(TILE_ROWS, TILE_COLS),
            scratch_shapes=[pltpu.VMEM((2, ABLOCK, 128), F32)],
        ),
        out_shape=jax.ShapeDtypeStruct((TILE_ROWS, TILE_COLS), F32),
        name="surface",
    )(idx, incoming, base, wet)


def _shift(axis, to):
    return [(i, to(i)) for i in range(8 if axis == "ay" else 16)]


def _total(part):
    core = lax.axis_index("ay") % 2
    half = part.shape[0] // 2
    swap = _shift("ay", lambda i: i ^ 1)
    first, second = part[:half], part[half:]
    mine = jnp.where(core == 0, first, second)
    theirs = jnp.where(core == 0, second, first)
    mine = mine + lax.ppermute(theirs, "ay", swap)
    for axis, to in (
        ("ay", lambda d: lambda i: (i + 2 * d) % 8),
        ("ax", lambda d: lambda i: (i + 4 * d) % 16),
        ("ax", lambda d: lambda i: i // 4 * 4 + (i + d) % 4),
    ):
        others = [lax.ppermute(mine, axis, _shift(axis, to(d))) for d in (1, 3, 2)]
        mine = mine + others[0] + others[1] + others[2]
    theirs = lax.ppermute(mine, "ay", swap)
    return jnp.concatenate([jnp.where(core == 0, mine, theirs), jnp.where(core == 0, theirs, mine)], axis=0)


def body(
    gaseous_model,
    forcing_boundary,
    relaxation_strength_profile,
    bottom_exchange_aloft,
    exchange_bottom_sensitivity,
    terrain_skin_warmth,
    tile_processor_home,
    marine_place_warmth,
    warming_coefficient,
):
    basis, fwd, back, synth, turn = (jnp.asarray(t) for t in _tables())
    ay, ax = lax.axis_index("ay"), lax.axis_index("ax")
    dev = jnp.reshape(ay * N_AX + ax, (1,)).astype(jnp.int32)
    pos = jnp.stack([ay, ax]).astype(jnp.int32)
    owners = tile_processor_home.reshape(DEVICES, 128)
    message, idx, wet = _pack(
        dev,
        exchange_bottom_sensitivity,
        owners,
        tile_processor_home.reshape(DEVICES, 1, 128),
        bottom_exchange_aloft,
        gaseous_model,
        marine_place_warmth,
        back,
    )
    incoming = lax.all_to_all(
        message.reshape(DEVICES, 2 * MSG_ROWS, 128), ("ay", "ax"), split_axis=0, concat_axis=0, tiled=True
    ).reshape(2 * DEVICES, MSG_ROWS, 128)
    pos, _ = lax.optimization_barrier((pos, idx))
    part = _analyse(pos, gaseous_model, forcing_boundary, basis)
    coef = _total(part)
    state, base = _nudge(
        pos,
        relaxation_strength_profile,
        exchange_bottom_sensitivity,
        warming_coefficient,
        coef,
        basis,
        gaseous_model,
        bottom_exchange_aloft,
        terrain_skin_warmth,
        wet,
    )
    incr = _held(idx, relaxation_strength_profile, coef, basis, synth, turn, fwd)
    flux, sst = _ocean(
        idx, exchange_bottom_sensitivity, warming_coefficient, incoming, incr, marine_place_warmth, fwd
    )
    surface = _surface(idx, incoming, base, wet)
    return state, flux, sst, surface


def solution(mesh):
    return jax.shard_map(
        body,
        mesh=mesh,
        in_specs=(
            P(None, "ay", "ax"),
            P(None, "ay", "ax"),
            P(),
            P(None, "ay", "ax"),
            P(),
            P("ay", "ax"),
            P(),
            P(("ay", "ax"), None),
            P(),
        ),
        out_specs=(
            P(None, "ay", "ax"),
            P(("ay", "ax"), None, None),
            P(("ay", "ax"), None),
            P("ay", "ax"),
        ),
        check_vma=False,
    )
```

time: 410 us -> 138 us (0.34); the launches traced: 403 us -> 137 us
  other arithmetic: 173 us -> 3.27 us
  local copies, waits for them, and re-layouts: 121 us -> 0 us
  Pallas kernels: 0 us -> 52.1 us
  matrix products: 26.7 us -> 0 us
  between operations: 14.7 us -> 0.7 us
  starting transfers between devices: 17.6 us -> 30.7 us
    scatter-add x1 -> x0, other arithmetic: 113 us -> none  [body(): jnp.nonzero(is_mine, size=processor_portion, fill_value=block_total)[0]]
    pallas_call x0 -> x6, Pallas kernels: none -> 52.1 us  [the longest x1 17.5 us: _pack(): pl.pallas_call(_pack_kernel, grid_spec=pltpu.PrefetchScalarGridSpec(num_s...]
    ppermute x0 -> x11, waiting for transfers between devices: none -> 49.8 us  [the longest x9 48 us: _total(): others = [lax.ppermute(mine, axis, _shift(axis, to(d))) for d in (1, 3, 2)]]
    all_gather x1 -> x0, waiting for transfers between devices: 40.9 us -> none  [over_pieces(): return lax.all_gather(value, axis).sum(0)]
    dot_general x6 -> x0, matrix products: 26.7 us -> none  [the longest x1 9.88 us: body(): jnp.dot(renewed_marine_warmth, return_matrix, precision=highest_accuracy,...]
    gather x8 -> x0, local copies, waits for them, and re-layouts: 23 us -> none  [the longest x1 11.6 us: body(): regridded[pick_rows]]
    select_n x10 -> x2, other arithmetic: 21.9 us -> 0.94 us  [the longest x1 0.93 us: _total(): theirs = jnp.where(core == 0, second, first)]
    mul x2 -> x0, local copies, waits for them, and re-layouts: 20.6 us -> none  [the longest x1 20.6 us: kron_table(): paired = weights[:, None, :, None] * weights[None, :, None, :]]
  transfers between devices with their start and end apart: 3 -> 12, of which waited for: 2 -> 11; matrix products, arithmetic and copies ran while one was open for 52% -> 2% of each run, Pallas kernels for 0% -> 15%
where the time goes in v1:
time: 138 us; the launch traced here: 137 us
  Pallas kernels  52.1 us (38%)
  waiting for transfers between devices  49.8 us (36%)
  starting transfers between devices  30.7 us (22%)
  other arithmetic  3.27 us (2%)
    ppermute x9, waiting for transfers between devices, _total(): others = [lax.ppermute(mine, axis, _shift(axis, to(d))) for d in (1, 3, 2)]  48 us
    pallas_call x1, Pallas kernels, _pack(): pl.pallas_call(_pack_kernel, grid_spec=pltpu.PrefetchScalarGridSpec(num_s...  17.5 us
    ppermute x9, starting transfers between devices, _total(): others = [lax.ppermute(mine, axis, _shift(axis, to(d))) for d in (1, 3, 2)]  13.1 us
    all_to_all x1, starting transfers between devices, body(): lax.all_to_all(message.reshape(DEVICES, 2 * MSG_ROWS, 128), ('ay', 'ax'),...  11.9 us
    pallas_call x1, Pallas kernels, _ocean(): pl.pallas_call(_ocean_kernel, grid_spec=pltpu.PrefetchScalarGridSpec(num_...  9.87 us
    pallas_call x1, Pallas kernels, _analyse(): pl.pallas_call(_analyse_kernel, grid_spec=pltpu.PrefetchScalarGridSpec(nu...  7.69 us
    pallas_call x1, Pallas kernels, _held(): pl.pallas_call(_held_kernel, grid_spec=pltpu.PrefetchScalarGridSpec(num_s...  6.69 us
    pallas_call x1, Pallas kernels, _nudge(): pl.pallas_call(_nudge_kernel, grid_spec=pltpu.PrefetchScalarGridSpec(num_...  6.1 us
  transfers between devices with their start and end apart: 12, of which 11 were waited for; matrix products, arithmetic and copies ran while one was open for 2% of the time, Pallas kernels for 15%

profile of v1, /device:TPU:1, one launch (start us, length us, event | category | flops | bytes accessed | tf_op | source)
XLA Modules:
  0.0 136.6 jit_solution(7773311393193356651)
XLA Ops:
  0.6 17.5 %pack.1 = (bf16[256,72,128]{2,1,0:T(8,128)(2,1)}, s32[8,128]{1,0:T(8,128)}, f32[16,256]{1,0:T(8,128)}) custom-call(s32[1]{0:T(128)} %bitcast.2.dev_s, f32[8]{0:T(128)} %sens_s.5, s32[128,128]{1,0:T(8,128)} %bitcast.8, s32[128,1,128]{2,1,0:T(1,128)} %bitcast.9, bf16[8,512,256]{2,1,0:T(8,128)(2,1)} %air_r.3, f32[4,512,256]{2,1,0:T(8,128)} %model_r.3, ...), custom_call_target="tpu_custom_call" | custom-call | tf_op jit(solution)/shard_map/pack/pallas_call | solution.py:199
  18.1 11.9 %all-to-all-start = ((bf16[128,144,128]{2,1,0:T(8,128)(2,1)}), bf16[128,144,128]{2,1,0:T(8,128)(2,1)}, u32[]{:S(2)}, u32[]{:S(2)}) async-start(bf16[128,144,128]{2,1,0:T(8,128)(2,1)} %bitcast.7), calls=%async_computation | async-start | bytes 9437184 | tf_op jit(solution)/shard_map/all_to_all | solution.py:607
  30.0 0.7 pad_add_fusion.pos_s
  30.7 7.7 %analyse.1 = f32[288,128]{1,0:T(8,128)} custom-call(s32[2]{0:T(128)} %pad_add_fusion.pos_s, f32[4,512,256]{2,1,0:T(8,128)} %model_r.3, f32[4,512,256]{2,1,0:T(8,128)} %forcing_r.1, bf16[4096,128]{1,0:T(8,128)(2,1)} %constant.35.clone.rows_r.cols_r.basis_r, bf16[4096,128]{1,0:T(8,128)(2,1)} %constant.35.clone.rows_r.cols_r.basis_r), custom_call_target="tpu_custom_call" | custom-call | tf_op jit(solution)/shard_map/analyse/pallas_call | solution.py:253
  38.4 0.9 slice_select_fusion
  39.3 1.5 %collective-permute-start = (f32[144,128]{1,0:T(8,128)S(1)}, f32[144,128]{1,0:T(8,128)S(1)}, u32[]{:S(2)}, u32[]{:S(2)}) collective-permute-start(f32[144,128]{1,0:T(8,128)S(1)} %slice_select_fusion), channel_id=1, source_target_pairs={{0,16},{16,0},{32,48},{48,32},{64,80},{80,64},{96,112},{112,96},{1... | collective-permute-start | bytes 221192 | tf_op jit(solution)/shard_map/ppermute | solution.py:569
  40.8 0.9 collective-permute-done
  41.7 0.9 select_add_fusion
  42.6 1.9 %collective-permute-start.3 = (f32[144,128]{1,0:T(8,128)S(1)}, f32[144,128]{1,0:T(8,128)S(1)}, u32[]{:S(2)}, u32[]{:S(2)}) collective-permute-start(f32[144,128]{1,0:T(8,128)S(1)} %select_add_fusion), channel_id=1, source_target_pairs={{0,64},{16,80},{32,96},{48,112},{64,0},{80,16},{96,32},{112,48},{1... | collective-permute-start | bytes 221192 | tf_op jit(solution)/shard_map/ppermute | solution.py:575
  44.6 0.9 collective-permute-start.2
  45.4 0.6 collective-permute-start.1
  46.0 38.7 %collective-permute-done.3 = f32[144,128]{1,0:T(8,128)S(1)} collective-permute-done((f32[144,128]{1,0:T(8,128)S(1)}, f32[144,128]{1,0:T(8,128)S(1)}, u32[]{:S(2)}, u32[]{:S(2)}) %collective-permute-start.3) | collective-permute-done | bytes 73760 | tf_op jit(solution)/shard_map/ppermute | solution.py:575
  84.7 0.1 collective-permute-done.2
  84.8 1.4 %collective-permute-done.1 = f32[144,128]{1,0:T(8,128)S(1)} collective-permute-done((f32[144,128]{1,0:T(8,128)S(1)}, f32[144,128]{1,0:T(8,128)S(1)}, u32[]{:S(2)}, u32[]{:S(2)}) %collective-permute-start.1) | collective-permute-done | bytes 73760 | tf_op jit(solution)/shard_map/ppermute | solution.py:575
  86.2 2.7 %collective-permute-start.6 = (f32[144,128]{1,0:T(8,128)S(1)}, f32[144,128]{1,0:T(8,128)S(1)}, u32[]{:S(2)}, u32[]{:S(2)}) collective-permute-start(f32[144,128]{1,0:T(8,128)S(1)} %add_add_fusion.2), channel_id=1, source_target_pairs={{0,8},{1,9},{2,10},{3,11},{4,12},{5,13},{6,14},{7,15},{8,0},{9,1},... | collective-permute-start | bytes 221192 | tf_op jit(solution)/shard_map/ppermute | solution.py:575
  88.9 0.4 collective-permute-start.5
  89.3 1.1 collective-permute-start.4
  90.4 0.6 collective-permute-done.6
  91.0 1.8 %collective-permute-done.5 = f32[144,128]{1,0:T(8,128)S(1)} collective-permute-done((f32[144,128]{1,0:T(8,128)S(1)}, f32[144,128]{1,0:T(8,128)S(1)}, u32[]{:S(2)}, u32[]{:S(2)}) %collective-permute-start.5) | collective-permute-done | bytes 73760 | tf_op jit(solution)/shard_map/ppermute | solution.py:575
  92.8 1.0 collective-permute-done.4
  93.8 4.0 %collective-permute-start.9 = (f32[144,128]{1,0:T(8,128)S(1)}, f32[144,128]{1,0:T(8,128)S(1)}, u32[]{:S(2)}, u32[]{:S(2)}) collective-permute-start(f32[144,128]{1,0:T(8,128)S(1)} %add_add_fusion.1), channel_id=1, source_target_pairs={{0,2},{1,3},{2,0},{3,1},{4,6},{5,7},{6,4},{7,5},{8,10},{9,11},{10,... | collective-permute-start | bytes 221192 | tf_op jit(solution)/shard_map/ppermute | solution.py:575
  97.8 1.4 %collective-permute-start.8 = (f32[144,128]{1,0:T(8,128)S(1)}, f32[144,128]{1,0:T(8,128)S(1)}, u32[]{:S(2)}, u32[]{:S(2)}) collective-permute-start(f32[144,128]{1,0:T(8,128)S(1)} %add_add_fusion.1), channel_id=1, source_target_pairs={{0,3},{1,0},{2,1},{3,2},{4,7},{5,4},{6,5},{7,6},{8,11},{9,8},{10,9... | collective-permute-start | bytes 221192 | tf_op jit(solution)/shard_map/ppermute | solution.py:575
  99.2 0.1 collective-permute-start.7
  99.2 0.3 collective-permute-done.9
  99.5 1.5 %collective-permute-done.8 = f32[144,128]{1,0:T(8,128)S(1)} collective-permute-done((f32[144,128]{1,0:T(8,128)S(1)}, f32[144,128]{1,0:T(8,128)S(1)}, u32[]{:S(2)}, u32[]{:S(2)}) %collective-permute-start.8) | collective-permute-done | bytes 73760 | tf_op jit(solution)/shard_map/ppermute | solution.py:575
  101.1 2.6 %collective-permute-done.7 = f32[144,128]{1,0:T(8,128)S(1)} collective-permute-done((f32[144,128]{1,0:T(8,128)S(1)}, f32[144,128]{1,0:T(8,128)S(1)}, u32[]{:S(2)}, u32[]{:S(2)}) %collective-permute-start.7) | collective-permute-done | bytes 73760 | tf_op jit(solution)/shard_map/ppermute | solution.py:575
  103.7 4.4 %collective-permute-start.10 = (f32[144,128]{1,0:T(8,128)S(1)}, f32[144,128]{1,0:T(8,128)S(1)}, u32[]{:S(2)}, u32[]{:S(2)}) collective-permute-start(f32[144,128]{1,0:T(8,128)S(1)} %add_add_fusion), channel_id=1, source_target_pairs={{0,16},{16,0},{32,48},{48,32},{64,80},{80,64},{96,112},{112,96},{1... | collective-permute-start | bytes 221192 | tf_op jit(solution)/shard_map/ppermute | solution.py:577
  108.1 0.9 collective-permute-done.10
  109.0 0.7 pad_maximum_fusion.coef_r
  109.7 6.7 %held.1.refs_32_ = f32[128,2304]{1,0:T(8,128)} custom-call(s32[8,128]{1,0:T(8,128)} %get-tuple-element.12.idx_s, f32[4]{0:T(128)} %strength_s.3, f32[288,128]{1,0:T(8,128)} %pad_maximum_fusion.coef_r, bf16[4096,128]{1,0:T(8,128)(2,1)} %constant.35.clone.rows_r.cols_r.basis_r, bf16[256,256]{1,0:T(8,128)(2,1)} %constant.38.clone.synth_r, ...), custom_call_target="tpu_custom_call" | custom-call | tf_op jit(solution)/shard_map/held/pallas_call | solution.py:421
  116.4 6.1 %nudge.1 = (f32[4,512,256]{2,1,0:T(8,128)}, f32[512,256]{1,0:T(8,128)}) custom-call(s32[2]{0:T(128)} %pad_add_fusion.pos_s, f32[4]{0:T(128)} %strength_s.3, f32[8]{0:T(128)} %sens_s.5, f32[8]{0:T(128)} %warm_s.3, f32[288,128]{1,0:T(8,128)} %pad_maximum_fusion.coef_r, bf16[4096,128]{1,0:T(8,128)(2,1)} %constant.35.clone.rows_r.cols_r.basis_r, ...), custom_call_target="tpu_custom_call" | custom-call | tf_op jit(solution)/shard_map/nudge/pallas_call | solution.py:333
  122.5 0.0 all-to-all-done
  122.5 4.2 %surface.1 = f32[512,256]{1,0:T(8,128)} custom-call(s32[8,128]{1,0:T(8,128)} %get-tuple-element.12.idx_s, ...), custom_call_target="tpu_custom_call" | custom-call | tf_op jit(solution)/shard_map/surface/pallas_call | solution.py:540
  126.7 9.9 %ocean.1 = (bf16[128,8,2304]{2,1,0:T(8,128)(2,1)}, f32[128,2304]{1,0:T(8,128)}) custom-call(s32[8,128]{1,0:T(8,128)} %get-tuple-element.12.idx_s, f32[8]{0:T(128)} %sens_s.5, f32[8]{0:T(128)} %warm_s.3, ...), custom_call_target="tpu_custom_call" | custom-call | tf_op jit(solution)/shard_map/ocean/pallas_call | solution.py:504
  (4 shorter events, 0.1 us)
Async XLA Ops:
  18.1 104.3 %all-to-all-start = ((bf16[128,144,128]{2,1,0:T(8,128)(2,1)}), bf16[128,144,128]{2,1,0:T(8,128)(2,1)}, u32[]{:S(2)}, u32[]{:S(2)}) async-start(bf16[128,144,128]{2,1,0:T(8,128)(2,1)} %bitcast.7), calls=%async_computation | async-start | bytes 9437184 | tf_op jit(solution)/shard_map/all_to_all | solution.py:607
  39.3 2.4 %collective-permute-start = (f32[144,128]{1,0:T(8,128)S(1)}, f32[144,128]{1,0:T(8,128)S(1)}, u32[]{:S(2)}, u32[]{:S(2)}) collective-permute-start(f32[144,128]{1,0:T(8,128)S(1)} %slice_select_fusion), channel_id=1, source_target_pairs={{0,16},{16,0},{32,48},{48,32},{64,80},{80,64},{96,112},{112,96},{1... | collective-permute-start | bytes 221192 | tf_op jit(solution)/shard_map/ppermute | solution.py:569
  42.6 42.1 %collective-permute-start.3 = (f32[144,128]{1,0:T(8,128)S(1)}, f32[144,128]{1,0:T(8,128)S(1)}, u32[]{:S(2)}, u32[]{:S(2)}) collective-permute-start(f32[144,128]{1,0:T(8,128)S(1)} %select_add_fusion), channel_id=1, source_target_pairs={{0,64},{16,80},{32,96},{48,112},{64,0},{80,16},{96,32},{112,48},{1... | collective-permute-start | bytes 221192 | tf_op jit(solution)/shard_map/ppermute | solution.py:575
  44.6 40.2 %collective-permute-start.2 = (f32[144,128]{1,0:T(8,128)S(1)}, f32[144,128]{1,0:T(8,128)S(1)}, u32[]{:S(2)}, u32[]{:S(2)}) collective-permute-start(f32[144,128]{1,0:T(8,128)S(1)} %select_add_fusion), channel_id=1, source_target_pairs={{0,96},{16,112},{32,0},{48,16},{64,32},{80,48},{96,64},{112,80},{1... | collective-permute-start | bytes 221192 | tf_op jit(solution)/shard_map/ppermute | solution.py:575
  45.4 40.7 %collective-permute-start.1 = (f32[144,128]{1,0:T(8,128)S(1)}, f32[144,128]{1,0:T(8,128)S(1)}, u32[]{:S(2)}, u32[]{:S(2)}) collective-permute-start(f32[144,128]{1,0:T(8,128)S(1)} %select_add_fusion), channel_id=1, source_target_pairs={{0,32},{16,48},{32,64},{48,80},{64,96},{80,112},{96,0},{112,16},{1... | collective-permute-start | bytes 221192 | tf_op jit(solution)/shard_map/ppermute | solution.py:575
  86.2 4.8 %collective-permute-start.6 = (f32[144,128]{1,0:T(8,128)S(1)}, f32[144,128]{1,0:T(8,128)S(1)}, u32[]{:S(2)}, u32[]{:S(2)}) collective-permute-start(f32[144,128]{1,0:T(8,128)S(1)} %add_add_fusion.2), channel_id=1, source_target_pairs={{0,8},{1,9},{2,10},{3,11},{4,12},{5,13},{6,14},{7,15},{8,0},{9,1},... | collective-permute-start | bytes 221192 | tf_op jit(solution)/shard_map/ppermute | solution.py:575
  88.9 3.9 %collective-permute-start.5 = (f32[144,128]{1,0:T(8,128)S(1)}, f32[144,128]{1,0:T(8,128)S(1)}, u32[]{:S(2)}, u32[]{:S(2)}) collective-permute-start(f32[144,128]{1,0:T(8,128)S(1)} %add_add_fusion.2), channel_id=1, source_target_pairs={{0,12},{1,13},{2,14},{3,15},{4,0},{5,1},{6,2},{7,3},{8,4},{9,5},{1... | collective-permute-start | bytes 221192 | tf_op jit(solution)/shard_map/ppermute | solution.py:575
  89.3 4.4 %collective-permute-start.4 = (f32[144,128]{1,0:T(8,128)S(1)}, f32[144,128]{1,0:T(8,128)S(1)}, u32[]{:S(2)}, u32[]{:S(2)}) collective-permute-start(f32[144,128]{1,0:T(8,128)S(1)} %add_add_fusion.2), channel_id=1, source_target_pairs={{0,4},{1,5},{2,6},{3,7},{4,8},{5,9},{6,10},{7,11},{8,12},{9,13},{1... | collective-permute-start | bytes 221192 | tf_op jit(solution)/shard_map/ppermute | solution.py:575
  93.8 5.7 %collective-permute-start.9 = (f32[144,128]{1,0:T(8,128)S(1)}, f32[144,128]{1,0:T(8,128)S(1)}, u32[]{:S(2)}, u32[]{:S(2)}) collective-permute-start(f32[144,128]{1,0:T(8,128)S(1)} %add_add_fusion.1), channel_id=1, source_target_pairs={{0,2},{1,3},{2,0},{3,1},{4,6},{5,7},{6,4},{7,5},{8,10},{9,11},{10,... | collective-permute-start | bytes 221192 | tf_op jit(solution)/shard_map/ppermute | solution.py:575
  97.8 3.3 %collective-permute-start.8 = (f32[144,128]{1,0:T(8,128)S(1)}, f32[144,128]{1,0:T(8,128)S(1)}, u32[]{:S(2)}, u32[]{:S(2)}) collective-permute-start(f32[144,128]{1,0:T(8,128)S(1)} %add_add_fusion.1), channel_id=1, source_target_pairs={{0,3},{1,0},{2,1},{3,2},{4,7},{5,4},{6,5},{7,6},{8,11},{9,8},{10,9... | collective-permute-start | bytes 221192 | tf_op jit(solution)/shard_map/ppermute | solution.py:575
  99.2 4.5 %collective-permute-start.7 = (f32[144,128]{1,0:T(8,128)S(1)}, f32[144,128]{1,0:T(8,128)S(1)}, u32[]{:S(2)}, u32[]{:S(2)}) collective-permute-start(f32[144,128]{1,0:T(8,128)S(1)} %add_add_fusion.1), channel_id=1, source_target_pairs={{0,1},{1,2},{2,3},{3,0},{4,5},{5,6},{6,7},{7,4},{8,9},{9,10},{10,1... | collective-permute-start | bytes 221192 | tf_op jit(solution)/shard_map/ppermute | solution.py:575
  103.7 5.3 %collective-permute-start.10 = (f32[144,128]{1,0:T(8,128)S(1)}, f32[144,128]{1,0:T(8,128)S(1)}, u32[]{:S(2)}, u32[]{:S(2)}) collective-permute-start(f32[144,128]{1,0:T(8,128)S(1)} %add_add_fusion), channel_id=1, source_target_pairs={{0,16},{16,0},{32,48},{48,32},{64,80},{80,64},{96,112},{112,96},{1... | collective-permute-start | bytes 221192 | tf_op jit(solution)/shard_map/ppermute | solution.py:577

commit v2 on v1

--- a/solution.py
+++ b/solution.py
@@ -230,23 +230,57 @@
     )(dev, sens, owners, own, air, model, marine, back)
 
 
-def _analyse_kernel(pos_s, model_r, forcing_r, rows_r, cols_r, out_r):
-    d = forcing_r[0] - model_r[0]
-    hi, lo = _hilo(d)
-    along = _mm(hi, cols_r[...]) + _mm(lo, cols_r[...])
-    along = along + pltpu.roll(along, 64, 1)
-    mean = jnp.sum(d, axis=1, keepdims=True) * (1.0 / 64.0)
-    lane = lax.broadcasted_iota(jnp.int32, (TILE_ROWS, 128), 1)
-    along = jnp.where(lane < 64, along, jnp.where(lane == 64, mean, 0.0))
+def _analyse_kernel(pos_s, model_r, forcing_r, rows_r, cols_r, out_r, left_s, right_s, core_s, border_s):
+    l = pl.program_id(0)
+
+    @pl.when(l == 0)
+    def _():
+        left_s[0:128, :] = jnp.transpose(rows_r[...].astype(F32)).astype(BF16)
+        row = lax.broadcasted_iota(jnp.int32, (16, TILE_ROWS), 0)
+        left_s[128:144, :] = jnp.where(row == 0, 1.0 / 64.0, 0.0).astype(BF16)
+        right_s[:, 0:128] = cols_r[...]
+        lane = lax.broadcasted_iota(jnp.int32, (TILE_COLS, 128), 1)
+        right_s[:, 128:256] = jnp.where(lane == 0, 1.0 / 64.0, 0.0).astype(BF16)
+        border_s[...] = jnp.zeros_like(border_s)
+        core_s[...] = jnp.zeros_like(core_s)
+
+    hi, lo = _hilo(forcing_r[0] - model_r[0])
+    along = _mm(left_s[...], hi) + _mm(left_s[...], lo)
+    along = jnp.concatenate([along[0:64] + along[64:128], along[128:136]], axis=0)
     hi, lo = _hilo(along)
-    contract = (((0,), (0,)), ((), ()))
-    both = lax.dot_general(rows_r[...], hi, contract, preferred_element_type=F32) + lax.dot_general(
-        rows_r[...], lo, contract, preferred_element_type=F32
-    )
-    out_r[0:64, :] = both[0:64] + both[64:128]
-    mean = jnp.sum(along, axis=0, keepdims=True) * (1.0 / 64.0)
+    both = _mm(hi, right_s[...]) + _mm(lo, right_s[...])
+    modes = both[:, 0:128]
+    modes = modes + pltpu.roll(modes, 64, 1)
+    lane = lax.broadcasted_iota(jnp.int32, (CROWS, 128), 1)
+    means = jnp.broadcast_to(both[:, 128:129], (CROWS, 128))
+    half = lane // 64 == l % 2
+    at = pl.multiple_of(l // 2 * 64, 64)
+    core_s[pl.ds(at, 64), :] = jnp.where(half[0:64], modes[0:64], core_s[pl.ds(at, 64), :])
+    border_s[0:64, :] = jnp.where(lane[0:64] == l, means[0:64], border_s[0:64, :])
     row = lax.broadcasted_iota(jnp.int32, (8, 128), 0)
-    out_r[64:72, :] = jnp.where(row == 0, jnp.broadcast_to(mean, (8, 128)), 0.0)
+    old = border_s[64:72, :]
+    const = jnp.broadcast_to(modes[64:65], (8, 128))
+    corner = jnp.broadcast_to(means[64:65], (8, 128))
+    old = jnp.where((row == l // 2) & half[0:8], const, old)
+    border_s[64:72, :] = jnp.where((row == 2) & (lane[0:8] == l), corner, old)
+
+    @pl.when(l == LEVELS - 1)
+    def _():
+        out_r[pl.ds(0, 128, stride=2), :] = core_s[...]
+        out_r[pl.ds(1, 128, stride=2), :] = border_s[...]
+
+
+def _unpack(coef_r, level):
+    core = coef_r[pl.ds(128 * (level // 2), 64, stride=2), :]
+    border = coef_r[pl.ds(1, 72, stride=2), :]
+    lane = lax.broadcasted_iota(jnp.int32, (72, 128), 1)
+    here = lane // 64 == level % 2
+    core = jnp.where(here[0:64], core, 0.0)
+    core = core + pltpu.roll(core, 64, 1)
+    column = jnp.sum(jnp.where(lane == level, border, 0.0), axis=1, keepdims=True)
+    row = jnp.where(here, border, 0.0)
+    row = (row + pltpu.roll(row, 64, 1))[64 + level // 2 : 65 + level // 2]
+    return core, column[0:64], row, column[66:67]
 
 
 def _analyse(pos, model, forcing, basis):
@@ -261,9 +295,15 @@
                 pl.BlockSpec((TILE_ROWS, 128), lambda l, p: (p[0], 0)),
                 pl.BlockSpec((TILE_COLS, 128), lambda l, p: (p[1], 0)),
             ],
-            out_specs=pl.BlockSpec((CROWS, 128), lambda l, p: (l, 0)),
-        ),
-        out_shape=jax.ShapeDtypeStruct((LEVELS * CROWS, 128), F32),
+            out_specs=pl.BlockSpec((2 * DEVICES, 128), lambda l, p: (0, 0)),
+            scratch_shapes=[
+                pltpu.VMEM((144, TILE_ROWS), BF16),
+                pltpu.VMEM((TILE_COLS, 256), BF16),
+                pltpu.VMEM((128, 128), F32),
+                pltpu.VMEM((128, 128), F32),
+            ],
+        ),
+        out_shape=jax.ShapeDtypeStruct((2 * DEVICES, 128), F32),
         name="analyse",
     )(pos, model, forcing, basis, basis)
 
@@ -279,25 +319,22 @@
         contract = (((1,), (1,)), ((), ()))
         cols = cols_r[...]
         for l in range(LEVELS):
-            coef = coef_r[CROWS * l : CROWS * l + CROWS, :]
-            modes = jnp.where(lane < 64, coef, 0.0)
-            hi, lo = _hilo(modes + pltpu.roll(modes, 64, 1))
-            low, _ = _hilo(modes - jnp.where(lane < 64, hi.astype(F32), 0.0))
-            t = lax.dot_general(hi, cols, contract, preferred_element_type=F32) + lax.dot_general(
-                low, cols, contract, preferred_element_type=F32
-            )
-            mean = jnp.sum(jnp.where(lane == 64, coef, 0.0), axis=1, keepdims=True) * (1.0 / 64.0)
-            t = (t + mean) * strength_s[l]
-            hi, lo = _hilo(t[0:64])
+            modes, column, const, corner = _unpack(coef_r, l)
+            parts = []
+            for block, mean in ((modes, column), (jnp.broadcast_to(const, (8, 128)), corner)):
+                hi, lo = _hilo(block)
+                lo = jnp.where(lane[: block.shape[0]] < 64, lo.astype(F32), 0.0).astype(BF16)
+                t = lax.dot_general(hi, cols, contract, preferred_element_type=F32) + lax.dot_general(
+                    lo, cols, contract, preferred_element_type=F32
+                )
+                parts.append((t + mean * (1.0 / 64.0)) * strength_s[l])
+            hi, lo = _hilo(parts[0])
             cols_s[l, 0:64, :] = hi
             cols_s[l, 64:128, :] = hi
             cols_s[l, 128:192, :] = lo
-            cols_s[l, 192:256, :] = jnp.broadcast_to((t[64:72] * (1.0 / 64.0))[0:1], (64, TILE_COLS)).astype(BF16)
-            c = t[64:65] * (1.0 / 64.0)
-            chi, clo = _hilo(c)
+            hi, lo = _hilo(parts[1][0:1] * (1.0 / 64.0))
             r = lax.broadcasted_iota(jnp.int32, (64, TILE_COLS), 0)
-            full = jnp.where(r == 0, chi.astype(F32), jnp.where(r == 1, clo.astype(F32), 0.0))
-            cols_s[l, 192:256, :] = full.astype(BF16)
+            cols_s[l, 192:256, :] = jnp.where(r == 0, hi.astype(F32), jnp.where(r == 1, lo.astype(F32), 0.0)).astype(BF16)
 
     n = model_r.shape[1]
     rows = rows_r[...]
@@ -336,7 +373,7 @@
             num_scalar_prefetch=4,
             grid=(per,),
             in_specs=[
-                pl.BlockSpec((LEVELS * CROWS, 128), lambda i, *_: (0, 0)),
+                pl.BlockSpec((2 * DEVICES, 128), lambda i, *_: (0, 0)),
                 pl.BlockSpec((n, 128), lambda i, p, *_: (p[0] * per + i, 0)),
                 pl.BlockSpec((TILE_COLS, 128), lambda i, p, *_: (p[1], 0)),
                 pl.BlockSpec((LEVELS, n, TILE_COLS), lambda i, *_: (0, i, 0)),
@@ -366,17 +403,20 @@
 
 
 def _held_kernel(idx_s, strength_s, coef_r, basis_r, synth_r, turn_r, fwd_r, out_r, plain_s, other_s, mean_s, left_s, cell_s):
-    lane = lax.broadcasted_iota(jnp.int32, (CROWS, 128), 1)
-    coef = coef_r[...] * strength_s[LEVELS - 1]
-    modes = jnp.where(lane < 64, coef, 0.0)
-    modes = modes + pltpu.roll(modes, 64, 1)
-    swapped = jnp.where(lane % 64 < 32, pltpu.roll(modes, 96, 1), pltpu.roll(modes, 32, 1))
-    mean = jnp.sum(jnp.where(lane == 64, coef, 0.0), axis=1, keepdims=True) * (1.0 / 64.0)
-    mean = jnp.broadcast_to(mean, (CROWS, 128))
-    right = jnp.concatenate([modes, swapped, mean], axis=1)
-    hi, lo = _hilo(right[0:64])
+    lane = lax.broadcasted_iota(jnp.int32, (64, 128), 1)
+    strength = strength_s[LEVELS - 1]
+    modes, column, row, corner = _unpack(coef_r, LEVELS - 1)
+
+    def swap(x):
+        return jnp.where(lane[: x.shape[0]] % 64 < 32, pltpu.roll(x, 96, 1), pltpu.roll(x, 32, 1))
+
+    column = jnp.broadcast_to(column * (1.0 / 64.0), (64, 128))
+    right = jnp.concatenate([modes, swap(modes), column], axis=1) * strength
+    row = jnp.broadcast_to(row, (8, 128))
+    corner = jnp.broadcast_to(corner * (1.0 / 64.0), (8, 128))
+    const = jnp.concatenate([row, swap(row), corner], axis=1)[0:1] * (strength * (1.0 / 64.0))
+    hi, lo = _hilo(right)
     weights = jnp.concatenate([hi, hi, lo, jnp.zeros_like(lo)], axis=0)
-    const = right[64:65] * (1.0 / 64.0)
     chunk = 512
     for i in range(GRID // chunk):
         rows = basis_r[chunk * i : chunk * i + chunk, :]
@@ -424,7 +464,7 @@
             num_scalar_prefetch=2,
             grid=(1,),
             in_specs=[
-                pl.BlockSpec((CROWS, 128), lambda i, *_: (LEVELS - 1, 0)),
+                whole(2 * DEVICES, 128),
                 whole(GRID, 128),
                 whole(256, 256),
                 whole(128, 256),
@@ -555,27 +595,8 @@
     )(idx, incoming, base, wet)
 
 
-def _shift(axis, to):
-    return [(i, to(i)) for i in range(8 if axis == "ay" else 16)]
-
-
-def _total(part):
-    core = lax.axis_index("ay") % 2
-    half = part.shape[0] // 2
-    swap = _shift("ay", lambda i: i ^ 1)
-    first, second = part[:half], part[half:]
-    mine = jnp.where(core == 0, first, second)
-    theirs = jnp.where(core == 0, second, first)
-    mine = mine + lax.ppermute(theirs, "ay", swap)
-    for axis, to in (
-        ("ay", lambda d: lambda i: (i + 2 * d) % 8),
-        ("ax", lambda d: lambda i: (i + 4 * d) % 16),
-        ("ax", lambda d: lambda i: i // 4 * 4 + (i + d) % 4),
-    ):
-        others = [lax.ppermute(mine, axis, _shift(axis, to(d))) for d in (1, 3, 2)]
-        mine = mine + others[0] + others[1] + others[2]
-    theirs = lax.ppermute(mine, "ay", swap)
-    return jnp.concatenate([jnp.where(core == 0, mine, theirs), jnp.where(core == 0, theirs, mine)], axis=0)
+def _exchange(x):
+    return lax.all_to_all(x, ("ay", "ax"), split_axis=0, concat_axis=0, tiled=True)
 
 
 def body(
@@ -594,6 +615,8 @@
     dev = jnp.reshape(ay * N_AX + ax, (1,)).astype(jnp.int32)
     pos = jnp.stack([ay, ax]).astype(jnp.int32)
     owners = tile_processor_home.reshape(DEVICES, 128)
+    part = _analyse(pos, gaseous_model, forcing_boundary, basis)
+    part = _exchange(part.reshape(DEVICES, 2, 128))
     message, idx, wet = _pack(
         dev,
         exchange_bottom_sensitivity,
@@ -604,12 +627,11 @@
         marine_place_warmth,
         back,
     )
-    incoming = lax.all_to_all(
-        message.reshape(DEVICES, 2 * MSG_ROWS, 128), ("ay", "ax"), split_axis=0, concat_axis=0, tiled=True
-    ).reshape(2 * DEVICES, MSG_ROWS, 128)
-    pos, _ = lax.optimization_barrier((pos, idx))
-    part = _analyse(pos, gaseous_model, forcing_boundary, basis)
-    coef = _total(part)
+    total = jnp.broadcast_to(jnp.sum(part, axis=0, keepdims=True), (DEVICES, 2, 128))
+    coef = _exchange(total)
+    message, coef = lax.optimization_barrier((message, coef))
+    coef = coef.reshape(2 * DEVICES, 128)
+    incoming = _exchange(message.reshape(DEVICES, 2 * MSG_ROWS, 128)).reshape(2 * DEVICES, MSG_ROWS, 128)
     state, base = _nudge(
         pos,
         relaxation_strength_profile,

time: 138 us -> 135 us (0.978)
  blocking collectives: 0 us -> 21.5 us
  starting transfers between devices: 30.7 us -> 14.4 us
  waiting for transfers between devices: 49.8 us -> 44.7 us
  other arithmetic: 3.27 us -> 0.75 us
  Pallas kernels: 52.1 us -> 50.3 us
    ppermute x11 -> x0, waiting for transfers between devices: 49.8 us -> none  [the longest x9 48 us: _total(): others = [lax.ppermute(mine, axis, _shift(axis, to(d))) for d in (1, 3, 2)]]
    all_to_all x1 -> x2, waiting for transfers between devices: 0.01 us -> 44.7 us  [_exchange(): lax.all_to_all(x, ('ay', 'ax'), split_axis=0, concat_axis=0, tiled=True)]
    all_to_all x0 -> x1, blocking collectives: none -> 21.5 us  [_exchange(): lax.all_to_all(x, ('ay', 'ax'), split_axis=0, concat_axis=0, tiled=True)]
    ppermute x11 -> x0, starting transfers between devices: 18.9 us -> none  [the longest x9 13.1 us: _total(): others = [lax.ppermute(mine, axis, _shift(axis, to(d))) for d in (1, 3, 2)]]
    all_to_all x1 -> x2, starting transfers between devices: 11.9 us -> 14.4 us  [_exchange(): lax.all_to_all(x, ('ay', 'ax'), split_axis=0, concat_axis=0, tiled=True)]
    pallas_call x1, Pallas kernels: 7.69 us -> 5.5 us  [_analyse(): pl.pallas_call(_analyse_kernel, grid_spec=pltpu.PrefetchScalarGridSpec(nu...]
  transfers between devices with their start and end apart: 12 -> 2, of which waited for: 11 -> 1; matrix products, arithmetic and copies ran while one was open for 2% -> 0% of each run, Pallas kernels for 15% -> 23%
where the time goes in v2:
time: 135 us; the launch traced here: 134 us
  Pallas kernels  50.3 us (37%)
  waiting for transfers between devices  44.7 us (33%)
  blocking collectives  21.5 us (16%)
  starting transfers between devices  14.4 us (11%)
    all_to_all x2, waiting for transfers between devices, _exchange(): lax.all_to_all(x, ('ay', 'ax'), split_axis=0, concat_axis=0, tiled=True)  44.7 us
    all_to_all x1, blocking collectives, _exchange(): lax.all_to_all(x, ('ay', 'ax'), split_axis=0, concat_axis=0, tiled=True)  21.5 us
    pallas_call x1, Pallas kernels, _pack(): pl.pallas_call(_pack_kernel, grid_spec=pltpu.PrefetchScalarGridSpec(num_s...  17.5 us
    all_to_all x2, starting transfers between devices, _exchange(): lax.all_to_all(x, ('ay', 'ax'), split_axis=0, concat_axis=0, tiled=True)  14.4 us
    pallas_call x1, Pallas kernels, _ocean(): pl.pallas_call(_ocean_kernel, grid_spec=pltpu.PrefetchScalarGridSpec(num_...  10.2 us
    pallas_call x1, Pallas kernels, _held(): pl.pallas_call(_held_kernel, grid_spec=pltpu.PrefetchScalarGridSpec(num_s...  6.75 us
    pallas_call x1, Pallas kernels, _nudge(): pl.pallas_call(_nudge_kernel, grid_spec=pltpu.PrefetchScalarGridSpec(num_...  6.22 us
    pallas_call x1, Pallas kernels, _analyse(): pl.pallas_call(_analyse_kernel, grid_spec=pltpu.PrefetchScalarGridSpec(nu...  5.5 us
  transfers between devices with their start and end apart: 2, of which 1 were waited for; matrix products, arithmetic and copies ran while one was open for 0% of the time, Pallas kernels for 23%

profile of v2, /device:TPU:1, one launch (start us, length us, event | category | flops | bytes accessed | tf_op | source)
XLA Modules:
  0.0 133.7 jit_solution(15700932784756417044)
XLA Ops:
  0.6 0.6 pad_add_fusion.pos_s
  1.2 5.5 %analyse.1 = f32[256,128]{1,0:T(8,128)} custom-call(s32[2]{0:T(128)} %pad_add_fusion.pos_s, f32[4,512,256]{2,1,0:T(8,128)} %model_r.3, f32[4,512,256]{2,1,0:T(8,128)} %forcing_r.1, bf16[4096,128]{1,0:T(8,128)(2,1)} %constant.23.clone.rows_r.cols_r.basis_r, bf16[4096,128]{1,0:T(8,128)(2,1)} %constant.23.clone.rows_r.cols_r.basis_r), custom_call_target="tpu_custom_call" | custom-call | tf_op jit(solution)/shard_map/analyse/pallas_call | solution.py:287
  6.7 21.5 %all_to_all.15 = f32[128,2,128]{2,1,0:T(2,128)S(1)} all-to-all(f32[128,2,128]{2,1,0:T(2,128)} %bitcast.12), channel_id=1, replica_groups=mesh['ay'=8,'ax'=16] {'ay','ax'}, dimensions={0} | all-to-all | bytes 262144 | tf_op jit(solution)/shard_map/all_to_all | solution.py:599
  28.2 0.1 reduce_sum.9
  28.4 0.7 broadcast_in_dim.2
  29.1 4.2 %all-to-all-start.1 = ((f32[128,2,128]{2,1,0:T(2,128)}), f32[128,2,128]{2,1,0:T(2,128)S(1)}, u32[]{:S(2)}, u32[]{:S(2)}) async-start(f32[128,2,128]{2,1,0:T(2,128)} %broadcast_in_dim.2), calls=%async_computation.1 | async-start | bytes 262144 | tf_op jit(solution)/shard_map/all_to_all | solution.py:599
  33.3 17.5 %pack.1 = (bf16[256,72,128]{2,1,0:T(8,128)(2,1)}, s32[8,128]{1,0:T(8,128)}, f32[16,256]{1,0:T(8,128)}) custom-call(s32[1]{0:T(128)} %bitcast.2.dev_s, f32[8]{0:T(128)} %sens_s.5, s32[128,128]{1,0:T(8,128)} %bitcast.13, s32[128,1,128]{2,1,0:T(1,128)} %bitcast.14, bf16[8,512,256]{2,1,0:T(8,128)(2,1)} %air_r.3, f32[4,512,256]{2,1,0:T(8,128)} %model_r.3, ...), custom_call_target="tpu_custom_call" | custom-call | tf_op jit(solution)/shard_map/pack/pallas_call | solution.py:199
  50.7 0.0 all-to-all-done.1
  50.7 0.0 copy-start
  50.8 0.6 copy-done
  51.4 10.2 %all-to-all-start.2 = ((bf16[128,144,128]{2,1,0:T(8,128)(2,1)}), bf16[128,144,128]{2,1,0:T(8,128)(2,1)}, u32[]{:S(2)}, u32[]{:S(2)}) async-start(bf16[128,144,128]{2,1,0:T(8,128)(2,1)} %bitcast.9), calls=%async_computation.2 | async-start | bytes 9437184 | tf_op jit(solution)/shard_map/all_to_all | solution.py:599
  61.6 6.2 %nudge.1 = (f32[4,512,256]{2,1,0:T(8,128)}, f32[512,256]{1,0:T(8,128)}) custom-call(s32[2]{0:T(128)} %pad_add_fusion.pos_s, f32[4]{0:T(128)} %strength_s.3, f32[8]{0:T(128)} %sens_s.5, f32[8]{0:T(128)} %warm_s.3, f32[256,128]{1,0:T(8,128)} %bitcast.10, bf16[4096,128]{1,0:T(8,128)(2,1)} %constant.23.clone.rows_r.cols_r.basis_r, ...), custom_call_target="tpu_custom_call" | custom-call | tf_op jit(solution)/shard_map/nudge/pallas_call | solution.py:370
  67.8 6.7 %held.1.refs_32_ = f32[128,2304]{1,0:T(8,128)} custom-call(s32[8,128]{1,0:T(8,128)} %get-tuple-element.17.idx_s, f32[4]{0:T(128)} %strength_s.3, f32[256,128]{1,0:T(8,128)} %bitcast.11, bf16[4096,128]{1,0:T(8,128)(2,1)} %constant.23.clone.rows_r.cols_r.basis_r, bf16[256,256]{1,0:T(8,128)(2,1)} %constant.26.clone.synth_r, f32[128,256]{1,0:T(8,128)} %constant.27.clone.turn_r, ...), custom_call_target="tpu_custom_call" | custom-call | tf_op jit(solution)/shard_map/held/pallas_call | solution.py:461
  74.6 44.7 %all-to-all-done.2 = bf16[128,144,128]{2,1,0:T(8,128)(2,1)} async-done(((bf16[128,144,128]{2,1,0:T(8,128)(2,1)}), bf16[128,144,128]{2,1,0:T(8,128)(2,1)}, u32[]{:S(2)}, u32[]{:S(2)}) %all-to-all-start.2) | async-done | bytes 4718624 | tf_op jit(solution)/shard_map/all_to_all | solution.py:599
  119.3 4.2 %surface.1 = f32[512,256]{1,0:T(8,128)} custom-call(s32[8,128]{1,0:T(8,128)} %get-tuple-element.17.idx_s, ...), custom_call_target="tpu_custom_call" | custom-call | tf_op jit(solution)/shard_map/surface/pallas_call | solution.py:580
  123.5 10.2 %ocean.1 = (bf16[128,8,2304]{2,1,0:T(8,128)(2,1)}, f32[128,2304]{1,0:T(8,128)}) custom-call(s32[8,128]{1,0:T(8,128)} %get-tuple-element.17.idx_s, f32[8]{0:T(128)} %sens_s.5, f32[8]{0:T(128)} %warm_s.3, ...), custom_call_target="tpu_custom_call" | custom-call | tf_op jit(solution)/shard_map/ocean/pallas_call | solution.py:544
Async XLA Ops:
  29.1 21.7 %all-to-all-start.1 = ((f32[128,2,128]{2,1,0:T(2,128)}), f32[128,2,128]{2,1,0:T(2,128)S(1)}, u32[]{:S(2)}, u32[]{:S(2)}) async-start(f32[128,2,128]{2,1,0:T(2,128)} %broadcast_in_dim.2), calls=%async_computation.1 | async-start | bytes 262144 | tf_op jit(solution)/shard_map/all_to_all | solution.py:599
  50.7 0.7 copy-start
  51.4 67.8 %all-to-all-start.2 = ((bf16[128,144,128]{2,1,0:T(8,128)(2,1)}), bf16[128,144,128]{2,1,0:T(8,128)(2,1)}, u32[]{:S(2)}, u32[]{:S(2)}) async-start(bf16[128,144,128]{2,1,0:T(8,128)(2,1)} %bitcast.9), calls=%async_computation.2 | async-start | bytes 9437184 | tf_op jit(solution)/shard_map/all_to_all | solution.py:599
